TPU v7x, 32 devices: a whole 2x2x4 slice. The times are simulated.
32 devices in a mesh: data: 32 (over z, y, x, core).
Axes of the slice: x: 2, y: 2, z: 4, core: 2. Of those that a mesh axis runs over, the one named last changes fastest.
Arguments:
- h_a: bfloat16 [16384, 384], P('data')
- h_b: bfloat16 [16384, 384], P('data')
- w_one: bfloat16 [384, 2048], replicated
- w_two: bfloat16 [2048, 2048], replicated
- w_three: bfloat16 [2048, 2048], replicated
- gain_one: float32 [2048], replicated
- shift_one: float32 [2048], replicated
- gain_two: float32 [2048], replicated
- shift_two: float32 [2048], replicated
- lam_off: float32 [], replicated
Outputs:
- output 1: float32 [], replicated
- output 2: float32 [384, 2048], P('data')
- output 3: float32 [2048, 2048], P('data')
- output 4: float32 [2048, 2048], P('data')
- output 5: float32 [2048], replicated
- output 6: float32 [2048], replicated
- output 7: float32 [2048], replicated
- output 8: float32 [2048], replicated
All inputs are finite; a program needn't handle non-finite values.
Results may differ from a plain program's by a relative error of at most 0.00504156.
Values are sent between devices in bfloat16 or wider.
A program may use at most 1 GiB of HBM per device.

v0:
```python
import jax
import jax.numpy as jnp
from jax import lax
from jax.sharding import PartitionSpec as P

NORM_EPS = 1e-5
ROW_DIMS = (((0, 1), (0, 1)), ((), ()))
FIRST_DIMS = (((0,), (0,)), ((), ()))
LAST_DIMS = (((2,), (1,)), ((), ()))


def norm_forward(values, total_rows):
    col_sums = jnp.stack([jnp.sum(values, axis=1), jnp.sum(values * values, axis=1)])
    col_sums = lax.psum(col_sums, "data")
    col_mean = col_sums[0] / total_rows
    inv_std = lax.rsqrt(col_sums[1] / total_rows - col_mean * col_mean + NORM_EPS)
    return (values - col_mean[:, None, :]) * inv_std[:, None, :], inv_std


def norm_backward(grad_out, normed, inv_std, total_rows):
    col_sums = lax.psum(jnp.stack([jnp.sum(grad_out, axis=1), jnp.sum(grad_out * normed, axis=1)]), "data")
    grad_in = inv_std[:, None, :] * (grad_out - (col_sums[0][:, None, :] + normed * col_sums[1][:, None, :]) / total_rows)
    return grad_in, col_sums


def solution(mesh):
    shards = mesh.shape["data"]

    def local_step(h_a, h_b, w_one, w_two, w_three, gain_one, shift_one, gain_two, shift_two, lam_off):
        rows_dev = h_a.shape[0]
        total_rows = rows_dev * shards
        feat_rows = jnp.concatenate([h_a, h_b], axis=0)
        hidden_one = jnp.dot(feat_rows, w_one, preferred_element_type=jnp.float32).reshape(2, rows_dev, -1)
        normed_one, inv_one = norm_forward(hidden_one, total_rows)
        pre_one = gain_one * normed_one + shift_one
        act_one = jax.nn.relu(pre_one).astype(jnp.bfloat16)
        hidden_two = jnp.dot(act_one, w_two, preferred_element_type=jnp.float32)
        normed_two, inv_two = norm_forward(hidden_two, total_rows)
        pre_two = gain_two * normed_two + shift_two
        act_two = jax.nn.relu(pre_two).astype(jnp.bfloat16)
        proj_out = jnp.dot(act_two, w_three, preferred_element_type=jnp.float32)
        normed_out, inv_out = norm_forward(proj_out, total_rows)
        embed_pair = normed_out.astype(jnp.bfloat16)
        corr_part = lax.dot_general(embed_pair[0], embed_pair[1], FIRST_DIMS, preferred_element_type=jnp.float32)
        corr_mat = lax.psum(corr_part, "data") / total_rows
        feat_index = jnp.arange(corr_mat.shape[0])
        diag_mask = feat_index[:, None] == feat_index[None, :]
        diag_gap = 1.0 - corr_mat
        loss_total = jnp.sum(jnp.where(diag_mask, diag_gap * diag_gap, lam_off * corr_mat * corr_mat))
        grad_corr = jnp.where(diag_mask, -2.0 * diag_gap, 2.0 * lam_off * corr_mat)
        grad_scaled = (grad_corr / total_rows).astype(jnp.bfloat16)
        grad_embed_a = lax.dot_general(embed_pair[1], grad_scaled, (((1,), (1,)), ((), ())),
                                       preferred_element_type=jnp.float32)
        grad_embed_b = jnp.dot(embed_pair[0], grad_scaled, preferred_element_type=jnp.float32)
        grad_embed = jnp.stack([grad_embed_a, grad_embed_b])
        grad_proj = norm_backward(grad_embed, normed_out, inv_out, total_rows)[0].astype(jnp.bfloat16)
        grad_w_three = lax.psum_scatter(
            lax.dot_general(act_two, grad_proj, ROW_DIMS, preferred_element_type=jnp.float32),
            "data", scatter_dimension=0, tiled=True)
        grad_act_two = lax.dot_general(grad_proj, w_three, LAST_DIMS, preferred_element_type=jnp.float32)
        grad_pre_two = jnp.where(pre_two > 0, grad_act_two, 0.0)
        grad_hidden_two, sums_two = norm_backward(grad_pre_two, normed_two, inv_two, total_rows)
        grad_hidden_two = (gain_two * grad_hidden_two).astype(jnp.bfloat16)
        grad_w_two = lax.psum_scatter(
            lax.dot_general(act_one, grad_hidden_two, ROW_DIMS, preferred_element_type=jnp.float32),
            "data", scatter_dimension=0, tiled=True)
        grad_act_one = lax.dot_general(grad_hidden_two, w_two, LAST_DIMS, preferred_element_type=jnp.float32)
        grad_pre_one = jnp.where(pre_one > 0, grad_act_one, 0.0)
        grad_hidden_one, sums_one = norm_backward(grad_pre_one, normed_one, inv_one, total_rows)
        grad_hidden_one = (gain_one * grad_hidden_one).astype(jnp.bfloat16).reshape(2 * rows_dev, -1)
        grad_w_one = lax.psum_scatter(
            lax.dot_general(feat_rows, grad_hidden_one, FIRST_DIMS, preferred_element_type=jnp.float32),
            "data", scatter_dimension=0, tiled=True)
        return (loss_total, grad_w_one, grad_w_two, grad_w_three,
                jnp.sum(sums_one[1], axis=0), jnp.sum(sums_one[0], axis=0),
                jnp.sum(sums_two[1], axis=0), jnp.sum(sums_two[0], axis=0))

    row_spec = P("data", None)
    whole_mat = P(None, None)
    whole_vec = P(None)
    return jax.shard_map(
        local_step, mesh=mesh,
        in_specs=(row_spec, row_spec, whole_mat, whole_mat, whole_mat,
                  whole_vec, whole_vec, whole_vec, whole_vec, P()),
        out_specs=(P(), row_spec, row_spec, row_spec, whole_vec, whole_vec, whole_vec, whole_vec),
        check_vma=False)
```

profile of v0, /device:TPU:0, one launch (start us, length us, event | category | flops | bytes accessed | tf_op | source)
XLA Modules:
  0.0 979.1 jit_solution(15467230095009681371)
XLA Ops:
  16.0 42.1 %psum.49 = f32[2,2,2048]{2,1,0:T(2,128)S(1)} all-reduce(f32[2,2,2048]{2,1,0:T(2,128)S(1)} %pad_maximum_fusion.1), channel_id=1, replica_groups=mesh['data'=32] {'data'}, use_global_device_ids=true, to_apply=%region_2.0 | all-reduce | flops 8192 | bytes 65536 | tf_op jit(solution)/shard_map/psum | solution.py:14
  58.2 15.8 %fusion.36 = (f32[2,2048]{1,0:T(2,128)S(1)}, f32[2,2048]{1,0:T(2,128)S(1)}, f32[2,512,2048]{2,1,0:T(8,128)}) fusion(bf16[2048,2048]{1,0:T(8,128)(2,1)} %param.13, f32[1024,2048]{1,0:T(8,128)} %get-tuple-element.30, f32[2048]{0:T(1024)S(1)} %copy-done.13, f32[2,2048]{1,0:T(2,128)S(1)} %fusion.31, f32[2,2048]{1,0:T(2,128)S(1)} %fusion.32, f32[2048]{0:T(1024)S(1)} %copy-done.11), kind=kOutput, calls=%fused_computation.85 | convolution fusion | flops 8608800768 | bytes 25247744 | tf_op jit(solution)/shard_map/dot_general | solution.py:37
  74.0 40.3 %psum.50 = f32[2,2,2048]{2,1,0:T(2,128)S(1)} all-reduce(f32[2,2,2048]{2,1,0:T(2,128)S(1)} %pad_maximum_fusion.2), channel_id=1, replica_groups=mesh['data'=32] {'data'}, use_global_device_ids=true, to_apply=%region_5.6 | all-reduce | flops 8192 | bytes 65536 | tf_op jit(solution)/shard_map/psum | solution.py:14
  114.4 15.8 %fusion.35 = (f32[2,2048]{1,0:T(2,128)S(1)}, f32[2,2048]{1,0:T(2,128)S(1)}, f32[2,512,2048]{2,1,0:T(8,128)}) fusion(bf16[2048,2048]{1,0:T(8,128)(2,1)} %param.14, f32[2,512,2048]{2,1,0:T(8,128)} %get-tuple-element.31, f32[2048]{0:T(1024)S(1)} %copy-done.12, f32[2,2048]{1,0:T(2,128)S(1)} %fusion.26, f32[2,2048]{1,0:T(2,128)S(1)} %fusion.27, ...), kind=kOutput, calls=%fused_computation.84 | convolution fusion | flops 8608800768 | bytes 25247744 | tf_op jit(solution)/shard_map/dot_general | solution.py:41
  130.3 40.3 %psum.51 = f32[2,2,2048]{2,1,0:T(2,128)S(1)} all-reduce(f32[2,2,2048]{2,1,0:T(2,128)S(1)} %pad_maximum_fusion.3), channel_id=1, replica_groups=mesh['data'=32] {'data'}, use_global_device_ids=true, to_apply=%region_8.9 | all-reduce | flops 8192 | bytes 65536 | tf_op jit(solution)/shard_map/psum | solution.py:14
  177.2 8.1 fusion.17
  186.0 277.4 %all-reduce.4.cloned.1.call-done = f32[2048,2048]{1,0:T(8,128)} async-done(((f32[2048,2048]{1,0:T(8,128)}), f32[2048,2048]{1,0:T(8,128)}) %all-reduce.4.cloned.1.call-update) | async-done | bytes 16777232 | tf_op jit(solution)/shard_map/psum | solution.py:45
  463.3 12.4 %convolution_bitcast_fusion.3 = f32[1,512,2048]{2,1,0:T(8,128)} fusion(bf16[2,512,2048]{2,1,0:T(8,128)(2,1)} %copy-done.4, f32[2048,2048]{1,0:T(8,128)} %all-reduce.4.cloned.1.call-done, f32[]{:T(128)S(6)} %mul.190), kind=kOutput, calls=%fused_computation.38 | convolution fusion | flops 4328521728 | bytes 23068676 | tf_op jit(solution)/shard_map/dot_general | solution.py:52
  475.7 9.3 convolution_bitcast_fusion.2
  489.6 40.5 %psum.53 = f32[2,2,2048]{2,1,0:T(2,128)S(1)} all-reduce(f32[2,2,2048]{2,1,0:T(2,128)S(1)} %pad_maximum_fusion.4), channel_id=1, replica_groups=mesh['data'=32] {'data'}, use_global_device_ids=true, to_apply=%region_13.14 | all-reduce | flops 8192 | bytes 65536 | tf_op jit(solution)/shard_map/psum | solution.py:21
  530.2 7.1 multiply_convert_fusion.3
  539.2 14.8 %convolution_bitcast_fusion = f32[2048,2048]{1,0:T(8,128)} fusion(bf16[2,512,2048]{2,1,0:T(8,128)(2,1)S(1)} %multiply_convert_fusion.3, f32[2,512,2048]{2,1,0:T(8,128)} %get-tuple-element.31, f32[2048]{0:T(1024)S(1)} %copy-done.12, f32[2,2048]{1,0:T(2,128)S(1)} %fusion.26, f32[2,2048]{1,0:T(2,128)S(1)} %fusion.27, f32[2048]{0:T(1024)S(1)} %copy-done.10), kind=kOutput, calls=%fused_computation.3 | convolution fusion | flops 8602517504 | bytes 29409280 | tf_op jit(solution)/shard_map/dot_general | solution.py:58
  554.1 16.9 %fusion.34 = (f32[2,2048]{1,0:T(2,128)S(1)}, f32[2,2048]{1,0:T(2,128)S(1)}, f32[2,512,2048]{2,1,0:T(8,128)}) fusion(f32[2,2048]{1,0:T(2,128)S(1)} %fusion.26, f32[2,512,2048]{2,1,0:T(8,128)} %get-tuple-element.31, f32[2,2048]{1,0:T(2,128)S(1)} %fusion.27, bf16[2,512,2048]{2,1,0:T(8,128)(2,1)} %copy-done.3, bf16[2048,2048]{1,0:T(8,128)(2,1)} %param.14, ...), kind=kOutput, calls=%fused_computation.83 | convolution fusion | flops 8608800768 | bytes 29442048 | tf_op jit(solution)/shard_map/dot_general | solution.py:60
  571.0 43.3 %psum.54 = f32[2,2,2048]{2,1,0:T(2,128)S(1)} all-reduce(f32[2,2,2048]{2,1,0:T(2,128)S(1)} %pad_maximum_fusion.5), channel_id=1, replica_groups=mesh['data'=32] {'data'}, use_global_device_ids=true, to_apply=%region_16.17 | all-reduce | flops 8192 | bytes 65536 | tf_op jit(solution)/shard_map/psum | solution.py:21
  614.9 7.1 multiply_convert_fusion.2
  624.0 14.8 %convolution_bitcast_fusion.1 = f32[2048,2048]{1,0:T(8,128)} fusion(bf16[2,512,2048]{2,1,0:T(8,128)(2,1)S(1)} %multiply_convert_fusion.2, f32[1024,2048]{1,0:T(8,128)} %get-tuple-element.30, f32[2048]{0:T(1024)S(1)} %copy-done.13, f32[2,2048]{1,0:T(2,128)S(1)} %fusion.31, f32[2,2048]{1,0:T(2,128)S(1)} %fusion.32, f32[2048]{0:T(1024)S(1)} %copy-done.11), kind=kOutput, calls=%fused_computation.4 | convolution fusion | flops 8602517504 | bytes 29409280 | tf_op jit(solution)/shard_map/dot_general | solution.py:65
  638.8 16.9 %fusion.33 = (f32[2,2048]{1,0:T(2,128)S(1)}, f32[2,2048]{1,0:T(2,128)S(1)}, f32[2,512,2048]{2,1,0:T(8,128)}) fusion(f32[2,2048]{1,0:T(2,128)S(1)} %fusion.31, f32[2,2048]{1,0:T(2,128)S(1)} %fusion.32, f32[1024,2048]{1,0:T(8,128)} %get-tuple-element.30, bf16[2,512,2048]{2,1,0:T(8,128)(2,1)} %copy-done.5, bf16[2048,2048]{1,0:T(8,128)(2,1)} %param.13, ...), kind=kOutput, calls=%fused_computation.82 | convolution fusion | flops 8608800768 | bytes 29442048 | tf_op jit(solution)/shard_map/dot_general | solution.py:67
  655.7 43.3 %psum.55 = f32[2,2,2048]{2,1,0:T(2,128)S(1)} all-reduce(f32[2,2,2048]{2,1,0:T(2,128)S(1)} %pad_maximum_fusion.6), channel_id=1, replica_groups=mesh['data'=32] {'data'}, use_global_device_ids=true, to_apply=%region_19.20 | all-reduce | flops 8192 | bytes 65536 | tf_op jit(solution)/shard_map/psum | solution.py:21
  699.7 7.1 multiply_convert_fusion.1
  710.4 89.4 %fusion = f32[16,2048]{1,0:T(8,128)S(1)} fusion(f32[384,2048]{1,0:T(8,128)} %fusion.37), kind=kCustom, calls=%all-reduce-scatter | all-reduce-scatter fusion | flops 1048577 | bytes 3276800
  811.1 6.3 collective-permute-start.2
  828.0 8.8 select_reduce_fusion
  838.1 6.0 collective-permute-done.6
  848.7 123.4 %reduce-scatter.5.cloned.1.call-done = f32[64,2048]{1,0:T(8,128)} async-done(((f32[2048,2048]{1,0:T(8,128)}), f32[64,2048]{1,0:T(8,128)}) %reduce-scatter.5.cloned.1.call-update) | async-done | bytes 524304 | tf_op jit(solution)/shard_map/reduce_scatter | solution.py:64
  (78 shorter events, 56.6 us)
Async XLA Ops:
  7.2 3.2 copy-start
  7.2 50.9 %copy-start.11 = (f32[2048]{0:T(1024)S(1)}, f32[2048]{0:T(1024)}, u32[]{:S(2)}) copy-start(f32[2048]{0:T(1024)} %param.15) | copy-start | bytes 24580
  7.2 50.9 %copy-start.13 = (f32[2048]{0:T(1024)S(1)}, f32[2048]{0:T(1024)}, u32[]{:S(2)}) copy-start(f32[2048]{0:T(1024)} %param.16) | copy-start | bytes 24580
  7.2 456.1 %all-reduce.4.cloned.1.call-start = ((), (), s32[]{:S(2)}) async-start(), calls=%async_computation.2 | async-start | bytes 33554432 | tf_op jit(solution)/shard_map/psum | solution.py:45
  58.1 56.3 %copy-start.10 = (f32[2048]{0:T(1024)S(1)}, f32[2048]{0:T(1024)}, u32[]{:S(2)}) copy-start(f32[2048]{0:T(1024)} %param.17) | copy-start | bytes 24580
  58.1 56.3 %copy-start.12 = (f32[2048]{0:T(1024)S(1)}, f32[2048]{0:T(1024)}, u32[]{:S(2)}) copy-start(f32[2048]{0:T(1024)} %param.18) | copy-start | bytes 24580
  175.2 1.9 copy-start.4
  185.3 663.4 %reduce-scatter.7.cloned.1.call-start = ((), (), s32[]{:S(2)}) async-start(), calls=%async_computation.4 | async-start | bytes 17301504 | tf_op jit(solution)/shard_map/reduce_scatter | solution.py:57
  463.3 12.4 %copy-start.2 = (f32[2048,2048]{1,0:T(8,128)S(1)}, f32[2048,2048]{1,0:T(8,128)}, u32[]{:S(2)}) copy-start(f32[2048,2048]{1,0:T(8,128)} %all-reduce.4.cloned.1.call-done) | copy-start | bytes 50331652
  463.3 21.7 %slice-start = ((s8[8388608]{0:T(1024)(128)(4,1)}), s8[4194304]{0:T(1024)(128)(4,1)S(1)}, s32[]{:S(2)}) async-start(s8[8388608]{0:T(1024)(128)(4,1)} %bitcast.127), calls=%async_computation.5 | async-start | bytes 8388608
  475.7 9.3 slice-start.1
  537.3 1.9 copy-start.3
  554.0 418.1 %reduce-scatter.5.cloned.1.call-start = ((), (), s32[]{:S(2)}) async-start(), calls=%async_computation.3 | async-start | bytes 17301504 | tf_op jit(solution)/shard_map/reduce_scatter | solution.py:64
  622.0 2.0 copy-start.5
  699.7 7.2 copy-start.7
  799.8 21.8 %collective-permute-start = (f32[16,2048]{1,0:T(8,128)S(1)}, f32[16,2048]{1,0:T(8,128)S(1)}, u32[]{:S(2)}, u32[]{:S(2)}) collective-permute-start(f32[16,2048]{1,0:T(8,128)S(1)} %fusion), channel_id=1, source_target_pairs={{0,1},{1,2},{2,3},{3,4},{4,5},{5,6},{6,7},{7,8},{8,9},{9,10},{10,1... | collective-permute-start | bytes 393224
  804.8 19.9 %collective-permute-start.1 = (f32[16,2048]{1,0:T(8,128)S(1)}, f32[16,2048]{1,0:T(8,128)S(1)}, u32[]{:S(2)}, u32[]{:S(2)}) collective-permute-start(f32[16,2048]{1,0:T(8,128)S(1)} %fusion), channel_id=1, source_target_pairs={{0,2},{1,3},{2,4},{3,5},{4,6},{5,7},{6,8},{7,9},{8,10},{9,11},{10,... | collective-permute-start | bytes 393224
  809.8 8.9 collective-permute-start.7
  811.1 161.0 %copy-start.1 = (bf16[384,2048]{1,0:T(8,128)(2,1)S(1)}, bf16[384,2048]{1,0:T(8,128)(2,1)}, u32[]{:S(2)}) copy-start(bf16[384,2048]{1,0:T(8,128)(2,1)} %param.12) | copy-start | bytes 4718596
  811.1 25.6 %collective-permute-start.2 = (f32[16,2048]{1,0:T(8,128)S(1)}, f32[16,2048]{1,0:T(8,128)S(1)}, u32[]{:S(2)}, u32[]{:S(2)}) collective-permute-start(f32[16,2048]{1,0:T(8,128)S(1)} %fusion), channel_id=1, source_target_pairs={{0,3},{1,4},{2,5},{3,6},{4,7},{5,8},{6,9},{7,10},{8,11},{9,12},{10... | collective-permute-start | bytes 393224
  817.4 19.3 %collective-permute-start.3 = (f32[16,2048]{1,0:T(8,128)S(1)}, f32[16,2048]{1,0:T(8,128)S(1)}, u32[]{:S(2)}, u32[]{:S(2)}) collective-permute-start(f32[16,2048]{1,0:T(8,128)S(1)} %fusion), channel_id=1, source_target_pairs={{0,4},{1,5},{2,6},{3,7},{4,8},{5,9},{6,10},{7,11},{8,12},{9,13},{1... | collective-permute-start | bytes 393224
  818.7 18.0 %collective-permute-start.4 = (f32[16,2048]{1,0:T(8,128)S(1)}, f32[16,2048]{1,0:T(8,128)S(1)}, u32[]{:S(2)}, u32[]{:S(2)}) collective-permute-start(f32[16,2048]{1,0:T(8,128)S(1)} %fusion), channel_id=1, source_target_pairs={{0,5},{1,6},{2,7},{3,8},{4,9},{5,10},{6,11},{7,12},{8,13},{9,14},{... | collective-permute-start | bytes 393224
  821.6 15.2 %collective-permute-start.5 = (f32[16,2048]{1,0:T(8,128)S(1)}, f32[16,2048]{1,0:T(8,128)S(1)}, u32[]{:S(2)}, u32[]{:S(2)}) collective-permute-start(f32[16,2048]{1,0:T(8,128)S(1)} %fusion), channel_id=1, source_target_pairs={{0,6},{1,7},{2,8},{3,9},{4,10},{5,11},{6,12},{7,13},{8,14},{9,15},... | collective-permute-start | bytes 393224
  824.7 19.3 %collective-permute-start.6 = (f32[16,2048]{1,0:T(8,128)S(1)}, f32[16,2048]{1,0:T(8,128)}, u32[]{:S(2)}, u32[]{:S(2)}) collective-permute-start(f32[16,2048]{1,0:T(8,128)S(1)} %fusion), channel_id=1, source_target_pairs={{0,7},{1,8},{2,9},{3,10},{4,11},{5,12},{6,13},{7,14},{8,15},{9,16}... | collective-permute-start | bytes 393224
  (3 other events, 2.2 us)
Sparse Core Ops, SparseCore 0:
  185.4 277.8 all-reduce.3
  554.1 203.7 reduce-scatter.6
  760.8 211.3 reduce-scatter.4
where the time goes:
time: 994 us; the launch traced here: 979 us
  waiting for transfers between devices  407 us (41%)
  blocking collectives  339 us (34%)
  matrix products  134 us (13%)
  other arithmetic  40.8 us (4%)
  starting transfers between devices  28.2 us (3%)
  between operations  15.3 us (2%)
  local copies, waits for them, and re-layouts  14.8 us (1%)
    psum x1, waiting for transfers between devices, local_step(): corr_mat = lax.psum(corr_part, 'data') / total_rows  277 us
    psum x3, blocking collectives, norm_backward(): lax.psum(jnp.stack([jnp.sum(grad_out, axis=1), jnp.sum(grad_out * normed,...  127 us
    reduce_scatter x1, waiting for transfers between devices, local_step(): lax.psum_scatter(lax.dot_general(act_one, grad_hidden_two, ROW_DIMS, pref...  123 us
    psum x3, blocking collectives, norm_forward(): col_sums = lax.psum(col_sums, 'data')  123 us
    unnamed x1, blocking collectives  89.4 us
    unnamed x8, starting transfers between devices  28.1 us
  transfers between devices with their start and end apart: 11, of which 3 were waited for; matrix products, arithmetic and copies ran while one was open for 17% of the time, Pallas kernels for 0%

commit v1 on v0

v1 whole, which is shorter than its diff:
```python
import functools

import jax
import jax.numpy as jnp
from jax import lax
from jax.experimental import pallas as pl
from jax.experimental.pallas import tpu as pltpu
from jax.sharding import PartitionSpec as P

NORM_EPS = 1e-5
FIRST_DIMS = (((0,), (0,)), ((), ()))
LAST_DIMS = (((2,), (1,)), ((), ()))
MESH = pl.DeviceIdType.MESH
VMEM = pl.BlockSpec(memory_space=pltpu.VMEM)
AXIS = "data"
CHUNK = 256
HALF = 128
LIMIT = 60 * 1024 * 1024


def coords():
    me = lax.axis_index(AXIS)
    return me, me // 8, (me // 4) % 2, (me // 2) % 2, me % 2


def device_of(z, y, x, c):
    return ((z * 2 + y) * 2 + x) * 2 + c


def greet(peers):
    barrier = pltpu.get_barrier_semaphore()
    for peer in peers:
        pl.semaphore_signal(barrier, inc=1, device_id=(peer,), device_id_type=MESH)
    pl.semaphore_wait(barrier, len(peers))


def remote(src, dst, send_sem, recv_sem, peer):
    return pltpu.make_async_remote_copy(src_ref=src, dst_ref=dst, send_sem=send_sem, recv_sem=recv_sem,
                                        device_id=(peer,), device_id_type=MESH)


def params(collective_id):
    return pltpu.CompilerParams(collective_id=collective_id, has_side_effects=True, vmem_limit_bytes=LIMIT)


def sums_kernel(part_ref, out_ref, in_plane, own, in_line, total,
                send_a, recv_a, send_b, recv_b, send_c, recv_c):
    me = lax.axis_index(AXIS)
    z, q = me // 8, me % 8
    width = part_ref.shape[1] // 8

    def cols(k):
        return pl.ds(pl.multiple_of(k * width, width), width)

    plane = [(q + d) % 8 for d in range(1, 8)]
    line = [(z + d) % 4 for d in range(1, 4)]
    greet([z * 8 + p for p in plane] + [p * 8 + q for p in line])
    first = [remote(part_ref.at[:, cols(p)], in_plane.at[d], send_a.at[d], recv_a.at[d], z * 8 + p)
             for d, p in enumerate(plane)]
    for copy in first:
        copy.start()
    acc = part_ref[:, cols(q)]
    for d, copy in enumerate(first):
        copy.wait()
        acc = acc + in_plane[d]
    own[...] = acc
    in_line[z] = acc
    second = [remote(own, in_line.at[z], send_b.at[d], recv_b.at[d], p * 8 + q) for d, p in enumerate(line)]
    for copy in second:
        copy.start()
    for copy in second:
        copy.wait()
    acc = (in_line[0] + in_line[1]) + (in_line[2] + in_line[3])
    total[...] = acc
    out_ref[:, cols(q)] = acc
    third = [remote(total, out_ref.at[:, cols(q)], send_c.at[d], recv_c.at[d], z * 8 + p)
             for d, p in enumerate(plane)]
    for copy in third:
        copy.start()
    for copy in third:
        copy.wait()


def all_sums(part, collective_id):
    rows, features = part.shape
    width = features // 8
    dma = pltpu.SemaphoreType.DMA
    return pl.pallas_call(
        sums_kernel,
        out_shape=jax.ShapeDtypeStruct((rows, features), jnp.float32),
        in_specs=[VMEM], out_specs=VMEM,
        scratch_shapes=[pltpu.VMEM((7, rows, width), jnp.float32), pltpu.VMEM((rows, width), jnp.float32),
                        pltpu.VMEM((4, rows, width), jnp.float32), pltpu.VMEM((rows, width), jnp.float32),
                        dma((7,)), dma((7,)), dma((3,)), dma((3,)), dma((7,)), dma((7,))],
        compiler_params=params(collective_id),
        name="all_sums",
    )(part)


def scatter_kernel(CHUNK, turned, lhs_ref, rhs_ref, out_ref, part, in_core, in_one_a, in_one_b, in_two_a, in_two_b, in_line,
                   sc, rc, s1a, r1a, s1b, r1b, s2a, r2a, s2b, r2b, s3, r3):
    me, z, y, x, c = coords()
    core_peer = device_of(z, y, x, 1 - c)
    x_peer = device_of(z, y, 1 - x, c)
    y_peer = device_of(z, 1 - y, x, c)
    line = [(z + d) % 4 for d in range(1, 4)]
    line_peers = [device_of(p, y, x, c) for p in line]
    chunks = rhs_ref.shape[1] // CHUNK
    rows = out_ref.shape[0]
    quarter = 8 * rows
    HALF = CHUNK // 2
    greet([core_peer, x_peer, y_peer] + line_peers)

    def both(j):
        return pl.ds(pl.multiple_of(j * CHUNK, CHUNK), CHUNK)

    def half_a(j):
        return pl.ds(pl.multiple_of(j * CHUNK, HALF), HALF)

    def half_b(j):
        return pl.ds(pl.multiple_of(j * CHUNK + HALF, HALF), HALF)

    def packed(j):
        return pl.ds(pl.multiple_of(j * HALF, HALF), HALF)

    def core_copy(j):
        return remote(part.at[:, :, :, 1 - c, :, both(j)], in_core.at[:, :, :, :, both(j)],
                      sc.at[j], rc.at[j], core_peer)

    def one_copies(j):
        return (remote(part.at[:, :, 1 - x, c, :, half_a(j)], in_one_a.at[:, :, :, packed(j)],
                       s1a.at[j], r1a.at[j], x_peer),
                remote(part.at[:, 1 - y, :, c, :, half_b(j)], in_one_b.at[:, :, :, packed(j)],
                       s1b.at[j], r1b.at[j], y_peer))

    def two_copies(j):
        return (remote(part.at[:, 1 - y, x, c, :, half_a(j)], in_two_a.at[:, :, packed(j)],
                       s2a.at[j], r2a.at[j], y_peer),
                remote(part.at[:, y, 1 - x, c, :, half_b(j)], in_two_b.at[:, :, packed(j)],
                       s2b.at[j], r2b.at[j], x_peer))

    def line_copies(j):
        return [remote(part.at[p, y, x, c, :, both(j)], in_line.at[d, :, both(j)],
                       s3.at[d, j], r3.at[d, j], line_peers[d]) for d, p in enumerate(line)]

    def step(t, carry):
        @pl.when(jnp.logical_and(t >= 4, t < chunks + 4))
        def _():
            j = t - 4
            copies = line_copies(j)
            for copy in copies:
                copy.wait()
            out_ref[:, both(j)] = ((part[z, y, x, c, :, both(j)] + in_line[0, :, both(j)])
                                   + (in_line[1, :, both(j)] + in_line[2, :, both(j)]))

        @pl.when(jnp.logical_and(t >= 3, t < chunks + 3))
        def _():
            j = t - 3
            for copy in two_copies(j):
                copy.wait()
            for w in range(4):
                part[w, y, x, c, :, half_a(j)] += in_two_a[w, :, packed(j)]
                part[w, y, x, c, :, half_b(j)] += in_two_b[w, :, packed(j)]
            for copy in line_copies(j):
                copy.start()

        @pl.when(jnp.logical_and(t >= 2, t < chunks + 2))
        def _():
            j = t - 2
            for copy in one_copies(j):
                copy.wait()
            for w in range(4):
                for v in range(2):
                    part[w, v, x, c, :, half_a(j)] += in_one_a[w, v, :, packed(j)]
                    part[w, y, v, c, :, half_b(j)] += in_one_b[w, v, :, packed(j)]
            for copy in two_copies(j):
                copy.start()

        @pl.when(jnp.logical_and(t >= 1, t < chunks + 1))
        def _():
            j = t - 1
            core_copy(j).wait()
            for w in range(4):
                for v in range(2):
                    for u in range(2):
                        part[w, v, u, c, :, both(j)] += in_core[w, v, u, :, both(j)]
            for copy in one_copies(j):
                copy.start()

        @pl.when(t < chunks)
        def _():
            rhs = rhs_ref[:, both(t)]

            def tile(w, carry):
                span = pl.ds(pl.multiple_of(w * quarter, quarter), quarter)
                if turned:
                    product = jnp.dot(lhs_ref[span, :], rhs, preferred_element_type=jnp.float32)
                else:
                    product = lax.dot_general(lhs_ref[:, span], rhs, FIRST_DIMS, preferred_element_type=jnp.float32)
                part[w, :, :, :, :, both(t)] = product.reshape(2, 2, 2, rows, CHUNK)
                return carry

            lax.fori_loop(0, 4, tile, 0)
            core_copy(t).start()

        return carry

    lax.fori_loop(0, chunks + 4, step, 0)


def product_scatter(lhs, rhs, collective_id, chunk=CHUNK, turned=False):
    total, depth = lhs.shape if turned else lhs.shape[::-1]
    features = rhs.shape[1]
    rows = total // 32
    chunks = features // chunk
    dma = pltpu.SemaphoreType.DMA
    f32 = jnp.float32
    return pl.pallas_call(
        functools.partial(scatter_kernel, chunk, turned),
        out_shape=jax.ShapeDtypeStruct((rows, features), f32),
        in_specs=[VMEM, VMEM], out_specs=VMEM,
        scratch_shapes=[pltpu.VMEM((4, 2, 2, 2, rows, features), f32), pltpu.VMEM((4, 2, 2, rows, features), f32),
                        pltpu.VMEM((4, 2, rows, features // 2), f32), pltpu.VMEM((4, 2, rows, features // 2), f32),
                        pltpu.VMEM((4, rows, features // 2), f32), pltpu.VMEM((4, rows, features // 2), f32),
                        pltpu.VMEM((3, rows, features), f32)]
                       + [dma((chunks,))] * 10 + [dma((3, chunks))] * 2,
        compiler_params=params(collective_id),
        cost_estimate=pl.CostEstimate(flops=2 * total * depth * features, bytes_accessed=4 * total * features,
                                      transcendentals=0),
        name="product_scatter",
    )(lhs, rhs)


def gather_kernel(block_ref, a_ref, b_ref, grad_a_ref, grad_b_ref, whole,
                  s3, r3, s2a, r2a, s2b, r2b, s1a, r1a, s1b, r1b, sc, rc):
    me, z, y, x, c = coords()
    core_peer = device_of(z, y, x, 1 - c)
    x_peer = device_of(z, y, 1 - x, c)
    y_peer = device_of(z, 1 - y, x, c)
    line = [(z + d) % 4 for d in range(1, 4)]
    line_peers = [device_of(p, y, x, c) for p in line]
    rows, features = block_ref.shape
    chunks = features // CHUNK
    greet([core_peer, x_peer, y_peer] + line_peers)

    def both(j):
        return pl.ds(pl.multiple_of(j * CHUNK, CHUNK), CHUNK)

    def half_a(j):
        return pl.ds(pl.multiple_of(j * CHUNK, HALF), HALF)

    def half_b(j):
        return pl.ds(pl.multiple_of(j * CHUNK + HALF, HALF), HALF)

    def line_copies(j):
        return [remote(block_ref.at[:, both(j)], whole.at[z, y, x, c, :, both(j)],
                       s3.at[d, j], r3.at[d, j], line_peers[d]) for d in range(3)]

    def two_copies(j):
        a, b = whole.at[:, y, x, c, :, half_a(j)], whole.at[:, y, x, c, :, half_b(j)]
        return (remote(a, a, s2a.at[j], r2a.at[j], y_peer), remote(b, b, s2b.at[j], r2b.at[j], x_peer))

    def one_copies(j):
        a, b = whole.at[:, :, x, c, :, half_a(j)], whole.at[:, y, :, c, :, half_b(j)]
        return (remote(a, a, s1a.at[j], r1a.at[j], x_peer), remote(b, b, s1b.at[j], r1b.at[j], y_peer))

    def core_copy(j):
        a = whole.at[:, :, :, c, :, both(j)]
        return remote(a, a, sc.at[j], rc.at[j], core_peer)

    whole[z, y, x, c] = block_ref[...]
    grad_a_ref[...] = jnp.zeros_like(grad_a_ref)

    def step(t, carry):
        @pl.when(t < chunks)
        def _():
            for copy in line_copies(t):
                copy.start()

        @pl.when(jnp.logical_and(t >= 1, t < chunks + 1))
        def _():
            for copy in line_copies(t - 1):
                copy.wait()
            for copy in two_copies(t - 1):
                copy.start()

        @pl.when(jnp.logical_and(t >= 2, t < chunks + 2))
        def _():
            for copy in two_copies(t - 2):
                copy.wait()
            for copy in one_copies(t - 2):
                copy.start()

        @pl.when(jnp.logical_and(t >= 3, t < chunks + 3))
        def _():
            for copy in one_copies(t - 3):
                copy.wait()
            core_copy(t - 3).start()

        @pl.when(t >= 4)
        def _():
            j = t - 4
            core_copy(j).wait()
            slab = whole[:, :, :, :, :, both(j)].reshape(32 * rows, CHUNK)
            grad_b_ref[:, both(j)] = jnp.dot(a_ref[...], slab, preferred_element_type=jnp.float32)
            grad_a_ref[...] += lax.dot_general(b_ref[:, both(j)], slab, (((1,), (1,)), ((), ())),
                                               preferred_element_type=jnp.float32)

        return carry

    lax.fori_loop(0, chunks + 4, step, 0)


def gather_products(block, embed_a, embed_b, collective_id):
    rows, features = block.shape
    chunks = features // CHUNK
    dma = pltpu.SemaphoreType.DMA
    shape = jax.ShapeDtypeStruct(embed_a.shape, jnp.float32)
    return pl.pallas_call(
        gather_kernel,
        out_shape=(shape, shape),
        in_specs=[VMEM] * 3, out_specs=(VMEM, VMEM),
        scratch_shapes=[pltpu.VMEM((4, 2, 2, 2, rows, features), jnp.bfloat16)]
                       + [dma((3, chunks))] * 2 + [dma((chunks,))] * 10,
        compiler_params=params(collective_id),
        cost_estimate=pl.CostEstimate(flops=4 * embed_a.size * features, bytes_accessed=4 * features * features,
                                      transcendentals=0),
        name="gather_products",
    )(block, embed_a, embed_b)


def norm_forward(values, total_rows, collective_id):
    part = jnp.concatenate([jnp.sum(values, axis=1), jnp.sum(values * values, axis=1)])
    col_sums = all_sums(part, collective_id).reshape(2, 2, -1)
    col_mean = col_sums[0] / total_rows
    inv_std = lax.rsqrt(col_sums[1] / total_rows - col_mean * col_mean + NORM_EPS)
    return (values - col_mean[:, None, :]) * inv_std[:, None, :], inv_std


def norm_backward(grad_out, normed, inv_std, total_rows, collective_id, extra=None):
    rows = [jnp.sum(grad_out, axis=1), jnp.sum(grad_out * normed, axis=1)]
    sums = all_sums(jnp.concatenate(rows if extra is None else rows + [extra]), collective_id)
    col_sums = sums[:4].reshape(2, 2, -1)
    grad_in = inv_std[:, None, :] * (grad_out - (col_sums[0][:, None, :] + normed * col_sums[1][:, None, :]) / total_rows)
    return grad_in, col_sums, sums[4:]


def solution(mesh):
    shards = mesh.shape[AXIS]

    def local_step(h_a, h_b, w_one, w_two, w_three, gain_one, shift_one, gain_two, shift_two, lam_off):
        me = lax.axis_index(AXIS)
        rows_dev = h_a.shape[0]
        total_rows = rows_dev * shards
        features = w_two.shape[0]
        feat_rows = jnp.concatenate([h_a, h_b], axis=0)
        in_rows = feat_rows.shape[1] // shards
        feat_t = jnp.pad(feat_rows.T.reshape(shards, in_rows, 2 * rows_dev), ((0, 0), (0, 16 - in_rows), (0, 0)))
        feat_t = feat_t.reshape(shards * 16, 2 * rows_dev)
        hidden_one = jnp.dot(feat_rows, w_one, preferred_element_type=jnp.float32).reshape(2, rows_dev, -1)
        normed_one, inv_one = norm_forward(hidden_one, total_rows, 0)
        pre_one = gain_one * normed_one + shift_one
        act_one = jax.nn.relu(pre_one).astype(jnp.bfloat16)
        hidden_two = jnp.dot(act_one, w_two, preferred_element_type=jnp.float32)
        normed_two, inv_two = norm_forward(hidden_two, total_rows, 1)
        pre_two = gain_two * normed_two + shift_two
        act_two = jax.nn.relu(pre_two).astype(jnp.bfloat16)
        proj_out = jnp.dot(act_two, w_three, preferred_element_type=jnp.float32)
        normed_out, inv_out = norm_forward(proj_out, total_rows, 2)
        embed_pair = normed_out.astype(jnp.bfloat16)
        corr_rows = product_scatter(embed_pair[0], embed_pair[1], 3) / total_rows
        block_rows = features // shards
        row_index = me * block_rows + jnp.arange(block_rows)
        diag_mask = row_index[:, None] == jnp.arange(features)[None, :]
        diag_gap = 1.0 - corr_rows
        loss_part = jnp.sum(jnp.where(diag_mask, diag_gap * diag_gap, lam_off * corr_rows * corr_rows),
                            axis=0, keepdims=True)
        grad_corr = jnp.where(diag_mask, -2.0 * diag_gap, 2.0 * lam_off * corr_rows)
        grad_scaled = (grad_corr / total_rows).astype(jnp.bfloat16)
        grad_embed = jnp.stack(gather_products(grad_scaled, embed_pair[0], embed_pair[1], 4))
        grad_proj, _, loss_row = norm_backward(grad_embed, normed_out, inv_out, total_rows, 5, loss_part)
        grad_proj = grad_proj.astype(jnp.bfloat16)
        loss_total = jnp.sum(loss_row)

        def flat(value):
            return value.reshape(2 * rows_dev, -1)

        grad_w_three = product_scatter(flat(act_two), flat(grad_proj), 6)
        grad_act_two = lax.dot_general(grad_proj, w_three, LAST_DIMS, preferred_element_type=jnp.float32)
        grad_pre_two = jnp.where(pre_two > 0, grad_act_two, 0.0)
        grad_hidden_two, sums_two, _ = norm_backward(grad_pre_two, normed_two, inv_two, total_rows, 7)
        grad_hidden_two = (gain_two * grad_hidden_two).astype(jnp.bfloat16)
        grad_w_two = product_scatter(flat(act_one), flat(grad_hidden_two), 8)
        grad_act_one = lax.dot_general(grad_hidden_two, w_two, LAST_DIMS, preferred_element_type=jnp.float32)
        grad_pre_one = jnp.where(pre_one > 0, grad_act_one, 0.0)
        grad_hidden_one, sums_one, _ = norm_backward(grad_pre_one, normed_one, inv_one, total_rows, 9)
        grad_hidden_one = (gain_one * grad_hidden_one).astype(jnp.bfloat16)
        grad_w_one = product_scatter(feat_t, flat(grad_hidden_one), 10, 512, True)[:in_rows]
        return (loss_total, grad_w_one, grad_w_two, grad_w_three,
                jnp.sum(sums_one[1], axis=0), jnp.sum(sums_one[0], axis=0),
                jnp.sum(sums_two[1], axis=0), jnp.sum(sums_two[0], axis=0))

    row_spec = P(AXIS, None)
    whole_mat = P(None, None)
    whole_vec = P(None)
    return jax.shard_map(
        local_step, mesh=mesh,
        in_specs=(row_spec, row_spec, whole_mat, whole_mat, whole_mat,
                  whole_vec, whole_vec, whole_vec, whole_vec, P()),
        out_specs=(P(), row_spec, row_spec, row_spec, whole_vec, whole_vec, whole_vec, whole_vec),
        check_vma=False)
```

time: 994 us -> 601 us (0.60); the launches traced: 979 us -> 597 us
  Pallas kernels: 0 us -> 453 us
  waiting for transfers between devices: 407 us -> 0 us
  blocking collectives: 339 us -> 0 us
  matrix products: 134 us -> 70.6 us
  starting transfers between devices: 28.2 us -> 0 us
  other arithmetic: 40.8 us -> 60.9 us
  between operations: 15.3 us -> 2.05 us
    pallas_call x0 -> x11, Pallas kernels: none -> 453 us  [the longest x4 316 us: product_scatter(): pl.pallas_call(functools.partial(scatter_kernel, chunk, turned), out_shap...]
    psum x1 -> x0, waiting for transfers between devices: 277 us -> none  [local_step(): corr_mat = lax.psum(corr_part, 'data') / total_rows]
    psum x6 -> x0, blocking collectives: 250 us -> none  [the longest x3 127 us: norm_backward(): lax.psum(jnp.stack([jnp.sum(grad_out, axis=1), jnp.sum(grad_out * normed,...]
    reduce_scatter x2 -> x0, waiting for transfers between devices: 123 us -> none  [the longest x1 123 us: local_step(): lax.psum_scatter(lax.dot_general(act_one, grad_hidden_two, ROW_DIMS, pref...]
    unnamed x1 -> x0, blocking collectives: 89.4 us -> none
    dot_general x6 -> x0, matrix products: 62.8 us -> none  [the longest x1 14.8 us: local_step(): lax.dot_general(act_two, grad_proj, ROW_DIMS, preferred_element_type=jnp....]
    unnamed x8 -> x0, starting transfers between devices: 28.1 us -> none
    convert_element_type x2 -> x5, other arithmetic: 14.2 us -> 29.6 us  [the longest x1 8.66 us: local_step(): grad_hidden_one = (gain_one * grad_hidden_one).astype(jnp.bfloat16)]
  transfers between devices with their start and end apart: 11 -> 0, of which waited for: 3 -> 0; matrix products, arithmetic and copies ran while one was open for 17% -> 0% of each run, Pallas kernels for 0% -> 0%
where the time goes in v1:
time: 601 us; the launch traced here: 597 us
  Pallas kernels  453 us (75%)
  matrix products  70.6 us (12%)
  other arithmetic  60.9 us (10%)
  local copies, waits for them, and re-layouts  10.4 us (2%)
    pallas_call x4, Pallas kernels, product_scatter(): pl.pallas_call(functools.partial(scatter_kernel, chunk, turned), out_shap...  316 us
    pallas_call x6, Pallas kernels, all_sums(): pl.pallas_call(sums_kernel, out_shape=jax.ShapeDtypeStruct((rows, feature...  85.2 us
    pallas_call x1, Pallas kernels, gather_products(): pl.pallas_call(gather_kernel, out_shape=(shape, shape), in_specs=[VMEM] *...  52.5 us
    dot_general x1, matrix products, local_step(): lax.dot_general(grad_proj, w_three, LAST_DIMS, preferred_element_type=jnp...  17.4 us
    dot_general x1, matrix products, local_step(): lax.dot_general(grad_hidden_two, w_two, LAST_DIMS, preferred_element_type...  16.9 us
    dot_general x1, matrix products, local_step(): hidden_two = jnp.dot(act_one, w_two, preferred_element_type=jnp.float32)  16 us
    dot_general x1, matrix products, local_step(): proj_out = jnp.dot(act_two, w_three, preferred_element_type=jnp.float32)  14.8 us

profile of v1, /device:TPU:0, one launch (start us, length us, event | category | flops | bytes accessed | tf_op | source)
XLA Modules:
  0.0 597.2 jit_solution(3554051996804550039)
XLA Ops:
  2.9 5.6 bitcast_reduce_fusion
  9.1 17.0 %all_sums.6 = f32[4,2048]{1,0:T(4,128)} custom-call(f32[4,2048]{1,0:T(4,128)} %pad_maximum_fusion.2.part_ref), custom_call_target="tpu_custom_call" | custom-call | tf_op jit(solution)/shard_map/all_sums/pallas_call | solution.py:88
  27.0 16.0 %fusion.29 = (f32[2,2048]{1,0:T(2,128)S(1)}, f32[2,2048]{1,0:T(2,128)S(1)}, f32[2,512,2048]{2,1,0:T(8,128)}) fusion(bf16[2048,2048]{1,0:T(8,128)(2,1)} %param.13, f32[1024,2048]{1,0:T(8,128)} %get-tuple-element.44, f32[2048]{0:T(1024)S(1)} %copy-done.9, f32[2,2048]{1,0:T(2,128)S(1)} %get-tuple-element.43, f32[2,2048]{1,0:T(2,128)S(1)} %get-tuple-element.42, ...), kind=kOutput, calls=%fused_computation.72 | convolution fusion | flops 8608800768 | bytes 25247744 | tf_op jit(solution)/shard_map/dot_general | solution.py:364
  43.7 13.4 %all_sums.7 = f32[4,2048]{1,0:T(4,128)} custom-call(f32[4,2048]{1,0:T(4,128)} %pad_maximum_fusion.3.part_ref), custom_call_target="tpu_custom_call" | custom-call | tf_op jit(solution)/shard_map/all_sums/pallas_call | solution.py:88
  57.9 4.9 maximum_convert_fusion
  62.8 14.8 %fusion.28 = (f32[2,2048]{1,0:T(2,128)S(1)}, f32[2,2048]{1,0:T(2,128)S(1)}, f32[2,512,2048]{2,1,0:T(8,128)}) fusion(bf16[2,512,2048]{2,1,0:T(8,128)(2,1)S(1)} %maximum_convert_fusion, bf16[2048,2048]{1,0:T(8,128)(2,1)} %param.14), kind=kOutput, calls=%fused_computation.71 | convolution fusion | flops 8596217856 | bytes 21004288 | tf_op jit(solution)/shard_map/dot_general | solution.py:368
  78.3 13.4 %all_sums.8 = f32[4,2048]{1,0:T(4,128)} custom-call(f32[4,2048]{1,0:T(4,128)} %pad_maximum_fusion.4.part_ref), custom_call_target="tpu_custom_call" | custom-call | tf_op jit(solution)/shard_map/all_sums/pallas_call | solution.py:88
  92.5 4.6 fusion.14
  97.1 2.3 slice_bitcast_fusion
  99.3 91.2 %product_scatter.4 = f32[64,2048]{1,0:T(8,128)} custom-call(bf16[512,2048]{1,0:T(8,128)(2,1)} %get-tuple-element.29.lhs_ref.a_ref, bf16[512,2048]{1,0:T(8,128)(2,1)} %get-tuple-element.28.rhs_ref.b_ref), custom_call_target="tpu_custom_call" | custom-call | flops 4294967296 | bytes 16777216 | tf_op jit(solution)/shard_map/product_scatter/pallas_call | solution.py:218
  193.3 52.5 %gather_products.1 = (f32[512,2048]{1,0:T(8,128)}, f32[512,2048]{1,0:T(8,128)}) custom-call(bf16[64,2048]{1,0:T(8,128)(2,1)} %get-tuple-element.30.block_ref, bf16[512,2048]{1,0:T(8,128)(2,1)} %get-tuple-element.29.lhs_ref.a_ref, bf16[512,2048]{1,0:T(8,128)(2,1)} %get-tuple-element.28.rhs_ref.b_ref), custom_call_target="tpu_custom_call" | custom-call | flops 8589934592 | bytes 16777216 | tf_op jit(solution)/shard_map/gather_products/pallas_call | solution.py:319
  245.8 7.0 %fusion.15 = (f32[2,2048]{1,0:T(2,128)S(1)}, f32[2,2048]{1,0:T(2,128)S(1)}) fusion(f32[1,512,2048]{2,1,0:T(8,128)} %bitcast.76, f32[1,512,2048]{2,1,0:T(8,128)} %bitcast.74, f32[2,2048]{1,0:T(2,128)S(1)} %get-tuple-element.39, f32[2,512,2048]{2,1,0:T(8,128)} %get-tuple-element.46, f32[2,2048]{1,0:T(2,128)S(1)} %get-tuple-element.38), kind=kLoop, calls=%fused_computation.37 | loop fusion | flops 12574720 | bytes 16842752 | tf_op jit(solution)/shard_map/reduce_sum | solution.py:341
  253.4 13.9 %all_sums.9 = f32[5,2048]{1,0:T(8,128)} custom-call(f32[5,2048]{1,0:T(8,128)} %pad_maximum_fusion.1.part_ref), custom_call_target="tpu_custom_call" | custom-call | tf_op jit(solution)/shard_map/all_sums/pallas_call | solution.py:88
  268.2 7.1 %multiply_convert_fusion.2 = bf16[2,512,2048]{2,1,0:T(8,128)(2,1)S(1)} fusion(f32[2,512,2048]{2,1,0:T(8,128)} %get-tuple-element.46, f32[1,512,2048]{2,1,0:T(8,128)} %bitcast.77, f32[1,512,2048]{2,1,0:T(8,128)} %bitcast.75, f32[2,2048]{1,0:T(2,128)S(1)} %get-tuple-element.33, f32[2,2048]{1,0:T(2,128)S(1)} %get-tuple-element.32, ...), kind=kLoop, calls=%fused_computation.24 | loop fusion | flops 18874368 | bytes 21037056 | tf_op jit(solution)/shard_map/convert_element_type | solution.py:382
  275.3 17.4 %fusion.27 = (f32[2,2048]{1,0:T(2,128)S(1)}, f32[2,2048]{1,0:T(2,128)S(1)}, f32[2,512,2048]{2,1,0:T(8,128)}) fusion(f32[2,2048]{1,0:T(2,128)S(1)} %get-tuple-element.41, f32[2,512,2048]{2,1,0:T(8,128)} %get-tuple-element.45, f32[2,2048]{1,0:T(2,128)S(1)} %get-tuple-element.40, bf16[2,512,2048]{2,1,0:T(8,128)(2,1)S(1)} %multiply_convert_fusion.2, ...), kind=kOutput, calls=%fused_computation.70 | convolution fusion | flops 8608800768 | bytes 29442048 | tf_op jit(solution)/shard_map/dot_general | solution.py:389
  293.3 13.4 %all_sums.10 = f32[4,2048]{1,0:T(4,128)} custom-call(f32[4,2048]{1,0:T(4,128)} %pad_maximum_fusion.5.part_ref), custom_call_target="tpu_custom_call" | custom-call | tf_op jit(solution)/shard_map/all_sums/pallas_call | solution.py:88
  308.3 9.0 %multiply_convert_fusion.1 = bf16[2,512,2048]{2,1,0:T(8,128)(2,1)} fusion(f32[2,512,2048]{2,1,0:T(8,128)} %get-tuple-element.47, f32[2,512,2048]{2,1,0:T(8,128)} %get-tuple-element.45, f32[2,2048]{1,0:T(2,128)S(1)} %get-tuple-element.34, f32[2,2048]{1,0:T(2,128)S(1)} %get-tuple-element.35, f32[2,2048]{1,0:T(2,128)S(1)} %get-tuple-element.41, ...), kind=kLoop, calls=%fused_computation.22 | loop fusion | flops 18874368 | bytes 21045248 | tf_op jit(solution)/shard_map/convert_element_type | solution.py:392
  317.2 6.9 %fusion.3.lhs_ref = bf16[1024,2048]{1,0:T(8,128)(2,1)} fusion(f32[1024,2048]{1,0:T(8,128)} %get-tuple-element.44, f32[2048]{0:T(1024)S(1)} %copy-done.9, f32[2048]{0:T(1024)S(1)} %copy-done.7, f32[2,2048]{1,0:T(2,128)S(1)} %get-tuple-element.43, f32[2,2048]{1,0:T(2,128)S(1)} %get-tuple-element.42), kind=kLoop, calls=%fused_computation.5 | loop fusion | flops 12582912 | bytes 12632064 | tf_op jit(solution)/shard_map/convert_element_type | solution.py:363
  324.1 92.9 %product_scatter.6 = f32[64,2048]{1,0:T(8,128)} custom-call(bf16[1024,2048]{1,0:T(8,128)(2,1)} %fusion.3.lhs_ref, bf16[1024,2048]{1,0:T(8,128)(2,1)} %bitcast.80), custom_call_target="tpu_custom_call" | custom-call | flops 8589934592 | bytes 16777216 | tf_op jit(solution)/shard_map/product_scatter/pallas_call | solution.py:218
  417.1 16.9 %fusion.26 = (f32[2,2048]{1,0:T(2,128)S(1)}, f32[2,2048]{1,0:T(2,128)S(1)}, f32[2,512,2048]{2,1,0:T(8,128)}) fusion(f32[2,2048]{1,0:T(2,128)S(1)} %get-tuple-element.43, f32[2,2048]{1,0:T(2,128)S(1)} %get-tuple-element.42, f32[1024,2048]{1,0:T(8,128)} %get-tuple-element.44, bf16[2,512,2048]{2,1,0:T(8,128)(2,1)} %multiply_convert_fusion.1, ...), kind=kOutput, calls=%fused_computation.69 | convolution fusion | flops 8608800768 | bytes 29442048 | tf_op jit(solution)/shard_map/dot_general | solution.py:394
  434.6 14.2 %all_sums.11 = f32[4,2048]{1,0:T(4,128)} custom-call(f32[4,2048]{1,0:T(4,128)} %pad_maximum_fusion.6.part_ref), custom_call_target="tpu_custom_call" | custom-call | tf_op jit(solution)/shard_map/all_sums/pallas_call | solution.py:88
  450.2 8.7 %multiply_convert_fusion = bf16[2,512,2048]{2,1,0:T(8,128)(2,1)} fusion(f32[2,512,2048]{2,1,0:T(8,128)} %get-tuple-element.48, f32[1024,2048]{1,0:T(8,128)} %get-tuple-element.44, f32[2,2048]{1,0:T(2,128)S(1)} %get-tuple-element.36, f32[2,2048]{1,0:T(2,128)S(1)} %get-tuple-element.37, f32[2,2048]{1,0:T(2,128)S(1)} %get-tuple-element.43, ...), kind=kLoop, calls=%fused_computation.20 | loop fusion | flops 18874368 | bytes 21045248 | tf_op jit(solution)/shard_map/convert_element_type | solution.py:397
  460.5 37.5 %product_scatter.5 = f32[16,2048]{1,0:T(8,128)} custom-call(bf16[512,1024]{1,0:T(8,128)(2,1)} %bitcast.83, bf16[1024,2048]{1,0:T(8,128)(2,1)} %bitcast.79), custom_call_target="tpu_custom_call" | custom-call | flops 2147483648 | bytes 4194304 | tf_op jit(solution)/shard_map/product_scatter/pallas_call | solution.py:218
  498.0 93.9 %product_scatter.7 = f32[64,2048]{1,0:T(8,128)} custom-call(bf16[1024,2048]{1,0:T(8,128)(2,1)} %bitcast.81, bf16[1024,2048]{1,0:T(8,128)(2,1)} %bitcast.78), custom_call_target="tpu_custom_call" | custom-call | flops 8589934592 | bytes 16777216 | tf_op jit(solution)/shard_map/product_scatter/pallas_call | solution.py:218
  (43 shorter events, 21.0 us)
Async XLA Ops:
  0.6 2.3 copy-start
  0.7 26.4 %copy-start.7 = (f32[2048]{0:T(1024)S(1)}, f32[2048]{0:T(1024)}, u32[]{:S(2)}) copy-start(f32[2048]{0:T(1024)} %param.15) | copy-start | bytes 24580
  0.7 26.4 %copy-start.9 = (f32[2048]{0:T(1024)S(1)}, f32[2048]{0:T(1024)}, u32[]{:S(2)}) copy-start(f32[2048]{0:T(1024)} %param.16) | copy-start | bytes 24580
  27.0 30.9 %copy-start.6 = (f32[2048]{0:T(1024)S(1)}, f32[2048]{0:T(1024)}, u32[]{:S(2)}) copy-start(f32[2048]{0:T(1024)} %param.17) | copy-start | bytes 24580
  27.0 30.9 %copy-start.8 = (f32[2048]{0:T(1024)S(1)}, f32[2048]{0:T(1024)}, u32[]{:S(2)}) copy-start(f32[2048]{0:T(1024)} %param.18) | copy-start | bytes 24580
  62.8 14.8 %copy-start.3 = (bf16[2,512,2048]{2,1,0:T(8,128)(2,1)}, bf16[2,512,2048]{2,1,0:T(8,128)(2,1)S(1)}, u32[]{:S(2)}) copy-start(bf16[2,512,2048]{2,1,0:T(8,128)(2,1)S(1)} %maximum_convert_fusion) | copy-start | bytes 12582916
  275.3 17.4 %copy-start.2 = (bf16[2,512,2048]{2,1,0:T(8,128)(2,1)}, bf16[2,512,2048]{2,1,0:T(8,128)(2,1)S(1)}, u32[]{:S(2)}) copy-start(bf16[2,512,2048]{2,1,0:T(8,128)(2,1)S(1)} %multiply_convert_fusion.2) | copy-start | bytes 12582916
  498.0 95.5 %copy-start.5 = (f32[16,2048]{1,0:T(8,128)S(1)}, f32[16,2048]{1,0:T(8,128)}, u32[]{:S(2)}) copy-start(f32[16,2048]{1,0:T(8,128)} %product_scatter.5) | copy-start | bytes 393220
  498.0 96.1 %copy-start.4 = (f32[64,2048]{1,0:T(8,128)S(1)}, f32[64,2048]{1,0:T(8,128)}, u32[]{:S(2)}) copy-start(f32[64,2048]{1,0:T(8,128)} %product_scatter.6) | copy-start | bytes 1572868
  498.0 98.8 %copy-start.1 = (bf16[384,2048]{1,0:T(8,128)(2,1)S(1)}, bf16[384,2048]{1,0:T(8,128)(2,1)}, u32[]{:S(2)}) copy-start(bf16[384,2048]{1,0:T(8,128)(2,1)} %param.12) | copy-start | bytes 4718596

commit v2 on v1

--- a/solution.py
+++ b/solution.py
@@ -9,7 +9,6 @@
 
 NORM_EPS = 1e-5
 FIRST_DIMS = (((0,), (0,)), ((), ()))
-LAST_DIMS = (((2,), (1,)), ((), ()))
 MESH = pl.DeviceIdType.MESH
 VMEM = pl.BlockSpec(memory_space=pltpu.VMEM)
 AXIS = "data"
@@ -327,6 +326,338 @@
                                       transcendentals=0),
         name="gather_products",
     )(block, embed_a, embed_b)
+
+
+DEEP = 4
+SLOTS = 3
+STREAM = 18
+BLOCK = 64
+
+
+def descent_kernel(top_ref, act_two_ref, act_one_ref, feat_ref, w_three_ref, w_two_ref, normed_two_ref, normed_one_ref, aux_ref,
+                   outs_ref, sums_ref,
+                   rows, acts, weights, normed, masked, part, in_core, in_one_a, in_one_b, in_two_a, in_two_b, in_line,
+                   part_sums, in_plane, own, in_rank, total,
+                   load_rows, load_acts, load_weights, load_normed,
+                   sc, rc, s1a, r1a, s1b, r1b, s2a, r2a, s2b, r2b, s3, r3,
+                   free_core, free_1a, free_1b, free_2a, free_2b, free_line,
+                   send_a, recv_a, send_b, recv_b, send_c, recv_c):
+    me, z, y, x, c = coords()
+    q = me % 8
+    core_peer = device_of(z, y, x, 1 - c)
+    x_peer = device_of(z, y, 1 - x, c)
+    y_peer = device_of(z, 1 - y, x, c)
+    line = [(z + d) % 4 for d in range(1, 4)]
+    line_peers = [device_of(p, y, x, c) for p in line]
+    line_sources = [device_of((z + 4 - d) % 4, y, x, c) for d in range(1, 4)]
+    plane = [(q + d) % 8 for d in range(1, 8)]
+    side = rows.shape[1] // 2
+    count = side * 32
+
+    copy_rows = pltpu.make_async_copy(top_ref, rows.at[0], load_rows)
+    copy_act_two = pltpu.make_async_copy(act_two_ref, acts, load_acts)
+    copy_act_one = pltpu.make_async_copy(act_one_ref, acts, load_acts)
+    copy_w_three = pltpu.make_async_copy(w_three_ref, weights, load_weights)
+    copy_w_two = pltpu.make_async_copy(w_two_ref, weights, load_weights)
+    copy_normed_two = pltpu.make_async_copy(normed_two_ref, normed, load_normed)
+    copy_normed_one = pltpu.make_async_copy(normed_one_ref, normed, load_normed)
+    for copy in (copy_rows, copy_act_two, copy_w_three, copy_normed_two):
+        copy.start()
+    greet([z * 8 + p for p in plane] + line_peers)
+    copy_rows.wait()
+
+    def both(j):
+        return pl.ds(pl.multiple_of(j * CHUNK, CHUNK), CHUNK)
+
+    def signal(sem, peer):
+        pl.semaphore_signal(sem, inc=1, device_id=(peer,), device_id_type=MESH)
+
+    low, high = pl.ds(0, HALF), pl.ds(HALF, HALF)
+
+    def core_copy(j):
+        return remote(part.at[j % DEEP, :, :, :, 1 - c], in_core.at[j % SLOTS], sc.at[j % SLOTS], rc.at[j % SLOTS], core_peer)
+
+    def one_copies(j):
+        p, s = j % DEEP, j % SLOTS
+        return (remote(part.at[p, :, :, 1 - x, c, :, low], in_one_a.at[s], s1a.at[s], r1a.at[s], x_peer),
+                remote(part.at[p, :, 1 - y, :, c, :, high], in_one_b.at[s], s1b.at[s], r1b.at[s], y_peer))
+
+    def two_copies(j):
+        p, s = j % DEEP, j % SLOTS
+        return (remote(part.at[p, :, 1 - y, x, c, :, low], in_two_a.at[s], s2a.at[s], r2a.at[s], y_peer),
+                remote(part.at[p, :, y, 1 - x, c, :, high], in_two_b.at[s], s2b.at[s], r2b.at[s], x_peer))
+
+    def line_copies(j):
+        p, s = j % DEEP, j % SLOTS
+        return [remote(part.at[p, w, y, x, c], in_line.at[s, d], s3.at[d, s], r3.at[d, s], line_peers[d])
+                for d, w in enumerate(line)]
+
+    def during(t, lag):
+        return pl.when(jnp.logical_and(t >= lag, t < STREAM + lag))
+
+    def stream_step(t):
+        @during(t, 4)
+        def _():
+            j = t - 4
+            p, s = j % DEEP, j % SLOTS
+            for copy in line_copies(j):
+                copy.wait()
+            outs_ref[j] = (part[p, z, y, x, c] + in_line[s, 0]) + (in_line[s, 1] + in_line[s, 2])
+
+            @pl.when(j < STREAM - SLOTS)
+            def _():
+                for d in range(3):
+                    signal(free_line.at[d], line_sources[d])
+
+        @during(t, 3)
+        def _():
+            j = t - 3
+            p, s = j % DEEP, j % SLOTS
+            for copy in two_copies(j):
+                copy.wait()
+            for w in range(4):
+                part[p, w, y, x, c, :, low] += in_two_a[s, w]
+                part[p, w, y, x, c, :, high] += in_two_b[s, w]
+
+            @pl.when(j < STREAM - SLOTS)
+            def _():
+                signal(free_2a, y_peer)
+                signal(free_2b, x_peer)
+
+            @pl.when(j >= SLOTS)
+            def _():
+                for d in range(3):
+                    pl.semaphore_wait(free_line.at[d], 1)
+
+            for copy in line_copies(j):
+                copy.start()
+
+        @during(t, 2)
+        def _():
+            j = t - 2
+            p, s = j % DEEP, j % SLOTS
+            for copy in one_copies(j):
+                copy.wait()
+            for w in range(4):
+                for v in range(2):
+                    part[p, w, v, x, c, :, low] += in_one_a[s, w, v]
+                    part[p, w, y, v, c, :, high] += in_one_b[s, w, v]
+
+            @pl.when(j < STREAM - SLOTS)
+            def _():
+                signal(free_1a, x_peer)
+                signal(free_1b, y_peer)
+
+            @pl.when(j >= SLOTS)
+            def _():
+                pl.semaphore_wait(free_2a, 1)
+                pl.semaphore_wait(free_2b, 1)
+
+            for copy in two_copies(j):
+                copy.start()
+
+        @during(t, 1)
+        def _():
+            j = t - 1
+            p, s = j % DEEP, j % SLOTS
+            core_copy(j).wait()
+            for w in range(4):
+                for v in range(2):
+                    for u in range(2):
+                        part[p, w, v, u, c] += in_core[s, w, v, u]
+
+            @pl.when(j < STREAM - SLOTS)
+            def _():
+                signal(free_core, core_peer)
+
+            @pl.when(j >= SLOTS)
+            def _():
+                pl.semaphore_wait(free_1a, 1)
+                pl.semaphore_wait(free_1b, 1)
+
+            for copy in one_copies(j):
+                copy.start()
+
+        @pl.when(t < 16)
+        def _():
+            rhs = rows[t // 8, :, both(t % 8)]
+
+            def tile(w, carry):
+                product = lax.dot_general(acts[:, pl.ds(pl.multiple_of(w * 512, 512), 512)], rhs, FIRST_DIMS,
+                                          preferred_element_type=jnp.float32)
+                part[t % DEEP, w] = product.reshape(2, 2, 2, BLOCK, CHUNK)
+                return carry
+
+            lax.fori_loop(0, 4, tile, 0)
+
+        @pl.when(jnp.logical_and(t >= 16, t < STREAM))
+        def _():
+            for k in range(4):
+                product = jnp.dot(feat_ref[...], rows[2, :, both((t - 16) * 4 + k)], preferred_element_type=jnp.float32)
+                part[t % DEEP, :, :, :, :, 16 * k:16 * k + 16, :] = product.reshape(4, 2, 2, 2, 16, CHUNK)
+
+        @pl.when(t < STREAM)
+        def _():
+            @pl.when(t >= SLOTS)
+            def _():
+                pl.semaphore_wait(free_core, 1)
+
+            core_copy(t).start()
+
+    def pull(layer, j):
+        cols = both(j)
+        gain, shift = aux_ref[layer, 0:1, cols], aux_ref[layer, 1:2, cols]
+        weight = weights[cols, :]
+        for view in range(2):
+            span = slice(view * side, (view + 1) * side)
+            grad = lax.dot_general(rows[layer, span, :], weight, (((1,), (1,)), ((), ())),
+                                   preferred_element_type=jnp.float32)
+            hat = normed[span, cols]
+            grad = jnp.where(gain * hat + shift > 0, grad, 0.0)
+            masked[span, cols] = grad
+            part_sums[view:view + 1, cols] = jnp.sum(grad, axis=0, keepdims=True)
+            part_sums[2 + view:3 + view, cols] = jnp.sum(grad * hat, axis=0, keepdims=True)
+
+    def push(layer, j):
+        cols = both(j)
+        gain = aux_ref[layer, 0:1, cols]
+        for view in range(2):
+            span = slice(view * side, (view + 1) * side)
+            inv = aux_ref[layer, 2 + view:3 + view, cols]
+            sum_one = sums_ref[layer, view:view + 1, cols] / count
+            sum_two = sums_ref[layer, 2 + view:3 + view, cols] / count
+            grad = inv * (masked[span, cols] - (sum_one + normed[span, cols] * sum_two))
+            rows[layer + 1, span, cols] = (gain * grad).astype(jnp.bfloat16)
+
+    def wide(k):
+        return pl.ds(pl.multiple_of(k * CHUNK, CHUNK), CHUNK)
+
+    def first_copies(layer):
+        return [remote(part_sums.at[:, wide(p)], in_plane.at[layer, d], send_a.at[d], recv_a.at[layer, d], z * 8 + p)
+                for d, p in enumerate(plane)]
+
+    def second_copies(layer):
+        return [remote(own, in_rank.at[layer, z], send_b.at[d], recv_b.at[layer, d], line_peers[d]) for d in range(3)]
+
+    def third_copies(layer):
+        return [remote(total, sums_ref.at[layer, :, wide(q)], send_c.at[d], recv_c.at[layer, d], z * 8 + p)
+                for d, p in enumerate(plane)]
+
+    def descend_step(t):
+        layer, phase = t // 8, t % 8
+
+        def at(k):
+            return pl.when(jnp.logical_and(t < 16, phase == k))
+
+        def pulls(lo, hi):
+            def body(j, carry):
+                pull(layer, j)
+                return carry
+            lax.fori_loop(lo, hi, body, 0)
+
+        def pushes(lo, hi):
+            def body(j, carry):
+                push(layer, j)
+                return carry
+            lax.fori_loop(lo, hi, body, 0)
+
+        @at(1)
+        def _():
+            copy_w_three.wait()
+            copy_normed_two.wait()
+            pulls(0, 2)
+
+        @at(2)
+        def _():
+            pulls(2, 5)
+
+        @at(3)
+        def _():
+            pulls(5, 8)
+            for copy in first_copies(layer):
+                copy.start()
+
+        @pl.when(t == 3)
+        def _():
+            copy_w_two.start()
+
+        @at(4)
+        def _():
+            acc = part_sums[:, wide(q)]
+            for d, copy in enumerate(first_copies(layer)):
+                copy.wait()
+                acc = acc + in_plane[layer, d]
+            own[...] = acc
+            in_rank[layer, z] = acc
+            for copy in second_copies(layer):
+                copy.start()
+
+        @at(5)
+        def _():
+            for copy in second_copies(layer):
+                copy.wait()
+            acc = (in_rank[layer, 0] + in_rank[layer, 1]) + (in_rank[layer, 2] + in_rank[layer, 3])
+            total[...] = acc
+            sums_ref[layer, :, wide(q)] = acc
+            for copy in third_copies(layer):
+                copy.start()
+
+        @at(6)
+        def _():
+            for copy in third_copies(layer):
+                copy.wait()
+            pushes(0, 4)
+
+        @at(7)
+        def _():
+            pushes(4, 8)
+
+        @pl.when(t == 7)
+        def _():
+            copy_act_one.start()
+            copy_normed_one.start()
+
+    def step(t, carry):
+        @pl.when(t == 0)
+        def _():
+            copy_act_two.wait()
+
+        @pl.when(t == 8)
+        def _():
+            copy_act_one.wait()
+
+        stream_step(t)
+        descend_step(t)
+        return carry
+
+    lax.fori_loop(0, STREAM + 4, step, 0)
+
+
+def descend(top, act_two, act_one, feat_t, w_three, w_two, normed_two, normed_one, aux, collective_id):
+    depth, features = top.shape
+    dma, regular = pltpu.SemaphoreType.DMA, pltpu.SemaphoreType.REGULAR
+    f32, bf16 = jnp.float32, jnp.bfloat16
+    away = pl.BlockSpec(memory_space=pltpu.HBM)
+    return pl.pallas_call(
+        descent_kernel,
+        out_shape=(jax.ShapeDtypeStruct((STREAM, BLOCK, CHUNK), f32), jax.ShapeDtypeStruct((2, 4, features), f32)),
+        in_specs=[away, away, away, VMEM, away, away, away, away, VMEM], out_specs=(VMEM, VMEM),
+        scratch_shapes=[pltpu.VMEM((3, depth, features), bf16), pltpu.VMEM((depth, features), bf16),
+                        pltpu.VMEM((features, features), bf16), pltpu.VMEM((depth, features), f32),
+                        pltpu.VMEM((depth, features), f32),
+                        pltpu.VMEM((DEEP, 4, 2, 2, 2, BLOCK, CHUNK), f32), pltpu.VMEM((SLOTS, 4, 2, 2, BLOCK, CHUNK), f32),
+                        pltpu.VMEM((SLOTS, 4, 2, BLOCK, HALF), f32), pltpu.VMEM((SLOTS, 4, 2, BLOCK, HALF), f32),
+                        pltpu.VMEM((SLOTS, 4, BLOCK, HALF), f32), pltpu.VMEM((SLOTS, 4, BLOCK, HALF), f32),
+                        pltpu.VMEM((SLOTS, 3, BLOCK, CHUNK), f32),
+                        pltpu.VMEM((4, features), f32), pltpu.VMEM((2, 7, 4, CHUNK), f32), pltpu.VMEM((4, CHUNK), f32),
+                        pltpu.VMEM((2, 4, 4, CHUNK), f32), pltpu.VMEM((4, CHUNK), f32)]
+                       + [dma] * 4 + [dma((SLOTS,))] * 10 + [dma((3, SLOTS))] * 2
+                       + [regular] * 5 + [regular((3,))]
+                       + [dma((7,)), dma((2, 7)), dma((3,)), dma((2, 3)), dma((7,)), dma((2, 7))],
+        compiler_params=pltpu.CompilerParams(collective_id=collective_id, has_side_effects=True,
+                                             vmem_limit_bytes=67043328),
+        name="descend",
+    )(top, act_two, act_one, feat_t, w_three, w_two, normed_two, normed_one, aux)
 
 
 def norm_forward(values, total_rows, collective_id):
@@ -385,20 +716,17 @@
         def flat(value):
             return value.reshape(2 * rows_dev, -1)
 
-        grad_w_three = product_scatter(flat(act_two), flat(grad_proj), 6)
-        grad_act_two = lax.dot_general(grad_proj, w_three, LAST_DIMS, preferred_element_type=jnp.float32)
-        grad_pre_two = jnp.where(pre_two > 0, grad_act_two, 0.0)
-        grad_hidden_two, sums_two, _ = norm_backward(grad_pre_two, normed_two, inv_two, total_rows, 7)
-        grad_hidden_two = (gain_two * grad_hidden_two).astype(jnp.bfloat16)
-        grad_w_two = product_scatter(flat(act_one), flat(grad_hidden_two), 8)
-        grad_act_one = lax.dot_general(grad_hidden_two, w_two, LAST_DIMS, preferred_element_type=jnp.float32)
-        grad_pre_one = jnp.where(pre_one > 0, grad_act_one, 0.0)
-        grad_hidden_one, sums_one, _ = norm_backward(grad_pre_one, normed_one, inv_one, total_rows, 9)
-        grad_hidden_one = (gain_one * grad_hidden_one).astype(jnp.bfloat16)
-        grad_w_one = product_scatter(feat_t, flat(grad_hidden_one), 10, 512, True)[:in_rows]
-        return (loss_total, grad_w_one, grad_w_two, grad_w_three,
-                jnp.sum(sums_one[1], axis=0), jnp.sum(sums_one[0], axis=0),
-                jnp.sum(sums_two[1], axis=0), jnp.sum(sums_two[0], axis=0))
+        aux = jnp.stack([jnp.stack([gain_two, shift_two, inv_two[0], inv_two[1]]),
+                         jnp.stack([gain_one, shift_one, inv_one[0], inv_one[1]])])
+        outs, sums = descend(flat(grad_proj), flat(act_two), flat(act_one), feat_t, w_three, w_two,
+                             flat(normed_two), flat(normed_one), aux, 6)
+
+        def block_of(chunk):
+            return chunk.transpose(1, 0, 2).reshape(block_rows, features)
+
+        grad_w_one = outs[16:].reshape(2, 4, 16, CHUNK).transpose(2, 0, 1, 3).reshape(16, features)[:in_rows]
+        return (loss_total, grad_w_one, block_of(outs[8:16]), block_of(outs[:8]),
+                sums[1, 2] + sums[1, 3], sums[1, 0] + sums[1, 1], sums[0, 2] + sums[0, 3], sums[0, 0] + sums[0, 1])
 
     row_spec = P(AXIS, None)
     whole_mat = P(None, None)

time: 601 us -> 489 us (0.81)
  Pallas kernels: 453 us -> 391 us
  matrix products: 70.6 us -> 37.7 us
  other arithmetic: 60.9 us -> 45.7 us
    pallas_call x4 -> x1, Pallas kernels: 316 us -> 91 us  [product_scatter(): pl.pallas_call(functools.partial(scatter_kernel, chunk, turned), out_shap...]
    pallas_call x0 -> x1, Pallas kernels: none -> 190 us  [descend(): pl.pallas_call(descent_kernel, out_shape=(jax.ShapeDtypeStruct((STREAM, B...]
    dot_general x2 -> x0, matrix products: 34.3 us -> none  [the longest x1 17.4 us: local_step(): lax.dot_general(grad_proj, w_three, LAST_DIMS, preferred_element_type=jnp...]
    pallas_call x6 -> x4, Pallas kernels: 85.2 us -> 57.8 us  [all_sums(): pl.pallas_call(sums_kernel, out_shape=jax.ShapeDtypeStruct((rows, feature...]
    convert_element_type x2 -> x0, other arithmetic: 17.6 us -> none  [the longest x1 8.96 us: local_step(): grad_hidden_two = (gain_two * grad_hidden_two).astype(jnp.bfloat16)]
where the time goes in v2:
time: 489 us; the launch traced here: 487 us
  Pallas kernels  391 us (80%)
  other arithmetic  45.7 us (9%)
  matrix products  37.7 us (8%)
  local copies, waits for them, and re-layouts  11.6 us (2%)
    pallas_call x1, Pallas kernels, descend(): pl.pallas_call(descent_kernel, out_shape=(jax.ShapeDtypeStruct((STREAM, B...  190 us
    pallas_call x1, Pallas kernels, product_scatter(): pl.pallas_call(functools.partial(scatter_kernel, chunk, turned), out_shap...  91 us
    pallas_call x4, Pallas kernels, all_sums(): pl.pallas_call(sums_kernel, out_shape=jax.ShapeDtypeStruct((rows, feature...  57.8 us
    pallas_call x1, Pallas kernels, gather_products(): pl.pallas_call(gather_kernel, out_shape=(shape, shape), in_specs=[VMEM] *...  52.5 us
    dot_general x1, matrix products, local_step(): hidden_two = jnp.dot(act_one, w_two, preferred_element_type=jnp.float32)  16 us
    dot_general x1, matrix products, local_step(): proj_out = jnp.dot(act_two, w_three, preferred_element_type=jnp.float32)  14.7 us

profile of v2, /device:TPU:0, one launch (start us, length us, event | category | flops | bytes accessed | tf_op | source)
XLA Modules:
  0.0 487.5 jit_solution(12605004365191292800)
XLA Ops:
  0.7 1.0 constant_dynamic-update-slice_fusion.1
  1.7 1.1 constant_dynamic-update-slice_fusion
  2.8 7.0 %bitcast_reduce_fusion = (f32[2,2048]{1,0:T(2,128)S(1)}, f32[2,2048]{1,0:T(2,128)S(1)}, f32[1024,2048]{1,0:T(8,128)}) fusion(bf16[1024,384]{1,0:T(8,128)(2,1)S(1)} %constant_dynamic-update-slice_fusion, bf16[384,2048]{1,0:T(8,128)(2,1)} %param.12), kind=kOutput, calls=%fused_computation.9 | convolution fusion | flops 1616896000 | bytes 10780672 | tf_op jit(solution)/shard_map/dot_general | solution.py:691
  10.4 17.0 %all_sums.4 = f32[4,2048]{1,0:T(4,128)} custom-call(f32[4,2048]{1,0:T(4,128)} %pad_maximum_fusion.3.part_ref), custom_call_target="tpu_custom_call" | custom-call | tf_op jit(solution)/shard_map/all_sums/pallas_call | solution.py:87
  28.3 16.0 %fusion.20 = (f32[2,2048]{1,0:T(2,128)S(1)}, f32[2,2048]{1,0:T(2,128)S(1)}, f32[2,512,2048]{2,1,0:T(8,128)}) fusion(bf16[2048,2048]{1,0:T(8,128)(2,1)} %w_two_ref.1, f32[1024,2048]{1,0:T(8,128)} %get-tuple-element.46, f32[2048]{0:T(1024)S(1)} %copy-done.3, f32[2,2048]{1,0:T(2,128)S(1)} %get-tuple-element.45, f32[2,2048]{1,0:T(2,128)S(1)} %get-tuple-element.44, ...), kind=kOutput, calls=%fused_computation.61 | convolution fusion | flops 8608800768 | bytes 25247744 | tf_op jit(solution)/shard_map/dot_general | solution.py:695
  44.9 13.4 %all_sums.5 = f32[4,2048]{1,0:T(4,128)} custom-call(f32[4,2048]{1,0:T(4,128)} %pad_maximum_fusion.4.part_ref), custom_call_target="tpu_custom_call" | custom-call | tf_op jit(solution)/shard_map/all_sums/pallas_call | solution.py:87
  59.2 6.6 %maximum_convert_fusion.1 = (bf16[2,512,2048]{2,1,0:T(8,128)(2,1)S(1)}, f32[2,512,2048]{2,1,0:T(8,128)}) fusion(f32[2048]{0:T(1024)S(1)} %copy-done.1, f32[2048]{0:T(1024)S(1)} %copy-done.2, f32[2,2048]{1,0:T(2,128)S(1)} %get-tuple-element.43, f32[2,512,2048]{2,1,0:T(8,128)} %get-tuple-element.47, f32[2,2048]{1,0:T(2,128)S(1)} %get-tuple-element.42), kind=kLoop, calls=%fused_computation.21 | loop fusion | flops 12582912 | bytes 21020672 | tf_op jit(solution)/shard_map/convert_element_type | solution.py:698
  65.8 14.7 %fusion.19 = (f32[2,2048]{1,0:T(2,128)S(1)}, f32[2,2048]{1,0:T(2,128)S(1)}, f32[2,512,2048]{2,1,0:T(8,128)}) fusion(bf16[2,512,2048]{2,1,0:T(8,128)(2,1)S(1)} %get-tuple-element.26, bf16[2048,2048]{1,0:T(8,128)(2,1)} %w_three_ref.1), kind=kOutput, calls=%fused_computation.60 | convolution fusion | flops 8596217856 | bytes 21004288 | tf_op jit(solution)/shard_map/dot_general | solution.py:699
  81.2 13.4 %all_sums.6 = f32[4,2048]{1,0:T(4,128)} custom-call(f32[4,2048]{1,0:T(4,128)} %pad_maximum_fusion.5.part_ref), custom_call_target="tpu_custom_call" | custom-call | tf_op jit(solution)/shard_map/all_sums/pallas_call | solution.py:87
  95.4 4.6 fusion.10
  100.0 2.3 slice_bitcast_fusion
  102.2 91.0 %product_scatter.1 = f32[64,2048]{1,0:T(8,128)} custom-call(bf16[512,2048]{1,0:T(8,128)(2,1)} %get-tuple-element.29.lhs_ref.a_ref, bf16[512,2048]{1,0:T(8,128)(2,1)} %get-tuple-element.28.rhs_ref.b_ref), custom_call_target="tpu_custom_call" | custom-call | flops 4294967296 | bytes 16777216 | tf_op jit(solution)/shard_map/product_scatter/pallas_call | solution.py:217
  193.9 2.0 multiply_convert_fusion.1
  195.9 52.5 %gather_products.1 = (f32[512,2048]{1,0:T(8,128)}, f32[512,2048]{1,0:T(8,128)}) custom-call(bf16[64,2048]{1,0:T(8,128)(2,1)} %get-tuple-element.32.block_ref, bf16[512,2048]{1,0:T(8,128)(2,1)} %get-tuple-element.29.lhs_ref.a_ref, bf16[512,2048]{1,0:T(8,128)(2,1)} %get-tuple-element.28.rhs_ref.b_ref), custom_call_target="tpu_custom_call" | custom-call | flops 8589934592 | bytes 16777216 | tf_op jit(solution)/shard_map/gather_products/pallas_call | solution.py:318
  248.4 7.0 %fusion.11 = (f32[2,2048]{1,0:T(2,128)S(1)}, f32[2,2048]{1,0:T(2,128)S(1)}) fusion(f32[1,512,2048]{2,1,0:T(8,128)} %bitcast.81, f32[1,512,2048]{2,1,0:T(8,128)} %bitcast.79, f32[2,2048]{1,0:T(2,128)S(1)} %get-tuple-element.41, f32[2,512,2048]{2,1,0:T(8,128)} %get-tuple-element.48, f32[2,2048]{1,0:T(2,128)S(1)} %get-tuple-element.40), kind=kLoop, calls=%fused_computation.25 | loop fusion | flops 12574720 | bytes 16842752 | tf_op jit(solution)/shard_map/reduce_sum | solution.py:672
  256.1 14.1 %all_sums.7 = f32[5,2048]{1,0:T(8,128)} custom-call(f32[5,2048]{1,0:T(8,128)} %pad_maximum_fusion.1.part_ref), custom_call_target="tpu_custom_call" | custom-call | tf_op jit(solution)/shard_map/all_sums/pallas_call | solution.py:87
  270.1 1.5 slice_reduce_fusion
  271.6 0.9 fusion.21
  272.5 8.8 %multiply_convert_fusion = bf16[2,512,2048]{2,1,0:T(8,128)(2,1)} fusion(f32[2,512,2048]{2,1,0:T(8,128)} %get-tuple-element.48, f32[1,512,2048]{2,1,0:T(8,128)} %bitcast.82, f32[1,512,2048]{2,1,0:T(8,128)} %bitcast.80, f32[2,2048]{1,0:T(2,128)S(1)} %get-tuple-element.39, f32[2,2048]{1,0:T(2,128)S(1)} %get-tuple-element.38, ...), kind=kLoop, calls=%fused_computation.17 | loop fusion | flops 18874368 | bytes 21037056 | tf_op jit(solution)/shard_map/convert_element_type | solution.py:713
  281.3 7.9 %maximum_convert_fusion = (bf16[1024,2048]{1,0:T(8,128)(2,1)}, f32[1024,2048]{1,0:T(8,128)}) fusion(f32[2048]{0:T(1024)S(1)} %copy-done.3, f32[2048]{0:T(1024)S(1)} %copy-done.4, f32[2,2048]{1,0:T(2,128)S(1)} %get-tuple-element.45, f32[1024,2048]{1,0:T(8,128)} %get-tuple-element.46, f32[2,2048]{1,0:T(2,128)S(1)} %get-tuple-element.44), kind=kLoop, calls=%fused_computation.16 | loop fusion | flops 12582912 | bytes 21020672 | tf_op jit(solution)/shard_map/convert_element_type | solution.py:694
  289.7 1.2 pad.4
  291.5 189.6 %descend.1 = (f32[18,64,256]{2,1,0:T(8,128)}, f32[2,4,2048]{2,1,0:T(4,128)}) custom-call(bf16[1024,2048]{1,0:T(8,128)(2,1)} %bitcast.77, bf16[1024,2048]{1,0:T(8,128)(2,1)} %bitcast.78, bf16[1024,2048]{1,0:T(8,128)(2,1)} %get-tuple-element.24.act_one_ref, bf16[512,1024]{1,0:T(8,128)(2,1)} %bitcast.83, bf16[2048,2048]{1,0:T(8,128)(2,1)} %w_three_ref.1, ...), custom_call_target="tpu_custom_call" | custom-call | tf_op jit(solution)/shard_map/descend/pallas_call | solution.py:641
  482.9 1.3 slice_bitcast_fusion.2
  485.9 1.6 slice_add_fusion
  (27 shorter events, 9.7 us)
Async XLA Ops:
  0.6 27.7 %copy-start.3 = (f32[2048]{0:T(1024)S(1)}, f32[2048]{0:T(1024)}, u32[]{:S(2)}) copy-start(f32[2048]{0:T(1024)} %param.16) | copy-start | bytes 24580
  0.6 27.7 %copy-start.4 = (f32[2048]{0:T(1024)S(1)}, f32[2048]{0:T(1024)}, u32[]{:S(2)}) copy-start(f32[2048]{0:T(1024)} %param.15) | copy-start | bytes 24580
  28.3 30.9 %copy-start.1 = (f32[2048]{0:T(1024)S(1)}, f32[2048]{0:T(1024)}, u32[]{:S(2)}) copy-start(f32[2048]{0:T(1024)} %param.18) | copy-start | bytes 24580
  28.3 30.9 %copy-start.2 = (f32[2048]{0:T(1024)S(1)}, f32[2048]{0:T(1024)}, u32[]{:S(2)}) copy-start(f32[2048]{0:T(1024)} %param.17) | copy-start | bytes 24580
  65.8 14.7 %copy-start = (bf16[2,512,2048]{2,1,0:T(8,128)(2,1)}, bf16[2,512,2048]{2,1,0:T(8,128)(2,1)S(1)}, u32[]{:S(2)}) copy-start(bf16[2,512,2048]{2,1,0:T(8,128)(2,1)S(1)} %get-tuple-element.26) | copy-start | bytes 12582916

commit v3 on v0

v3 whole, which is shorter than its diff:
```python
import jax
import jax.numpy as jnp
from jax import lax
from jax.experimental import pallas as pl
from jax.experimental.pallas import tpu as pltpu
from jax.sharding import PartitionSpec as P

NORM_EPS = 1e-5
FIRST_DIMS = (((0,), (0,)), ((), ()))
MESH = pl.DeviceIdType.MESH
VMEM = pl.BlockSpec(memory_space=pltpu.VMEM)
AXIS = "data"
CHUNK = 256
HALF = 128
LIMIT = 67043328
DEEP = 4
SLOTS = 3
STREAM = 18
BLOCK = 64


def coords():
    me = lax.axis_index(AXIS)
    return me, me // 8, (me // 4) % 2, (me // 2) % 2, me % 2


def device_of(z, y, x, c):
    return ((z * 2 + y) * 2 + x) * 2 + c


def greet(peers):
    barrier = pltpu.get_barrier_semaphore()
    for peer in peers:
        pl.semaphore_signal(barrier, inc=1, device_id=(peer,), device_id_type=MESH)
    pl.semaphore_wait(barrier, len(peers))


def remote(src, dst, send_sem, recv_sem, peer):
    return pltpu.make_async_remote_copy(src_ref=src, dst_ref=dst, send_sem=send_sem, recv_sem=recv_sem,
                                        device_id=(peer,), device_id_type=MESH)


def params(collective_id):
    return pltpu.CompilerParams(collective_id=collective_id, has_side_effects=True, vmem_limit_bytes=LIMIT)


def both(j):
    return pl.ds(pl.multiple_of(j * CHUNK, CHUNK), CHUNK)


def stream_scratch():
    dma, regular, f32 = pltpu.SemaphoreType.DMA, pltpu.SemaphoreType.REGULAR, jnp.float32
    return [pltpu.VMEM((DEEP, 4, 2, 2, 2, BLOCK, CHUNK), f32), pltpu.VMEM((SLOTS, 4, 2, 2, BLOCK, CHUNK), f32),
            pltpu.VMEM((SLOTS, 4, 2, BLOCK, HALF), f32), pltpu.VMEM((SLOTS, 4, 2, BLOCK, HALF), f32),
            pltpu.VMEM((SLOTS, 4, BLOCK, HALF), f32), pltpu.VMEM((SLOTS, 4, BLOCK, HALF), f32),
            pltpu.VMEM((SLOTS, 3, BLOCK, CHUNK), f32)] + [dma((SLOTS,))] * 10 + [dma((3, SLOTS))] * 2 \
        + [regular] * 5 + [regular((3,))]


STREAM_REFS = 25


def peers_of(spot):
    z, y, x, c = spot
    line = [(z + d) % 4 for d in range(1, 4)]
    return (device_of(z, y, x, 1 - c), device_of(z, y, 1 - x, c), device_of(z, 1 - y, x, c),
            line, [device_of(p, y, x, c) for p in line])


def stream_of(length, spot, refs, produce, consume):
    (part, in_core, in_one_a, in_one_b, in_two_a, in_two_b, in_line,
     sc, rc, s1a, r1a, s1b, r1b, s2a, r2a, s2b, r2b, s3, r3,
     free_core, free_1a, free_1b, free_2a, free_2b, free_line) = refs
    z, y, x, c = spot
    core_peer, x_peer, y_peer, line, line_peers = peers_of(spot)
    line_sources = [device_of((z + 4 - d) % 4, y, x, c) for d in range(1, 4)]
    low, high = pl.ds(0, HALF), pl.ds(HALF, HALF)

    def signal(sem, peer):
        pl.semaphore_signal(sem, inc=1, device_id=(peer,), device_id_type=MESH)

    def core_copy(j):
        return remote(part.at[j % DEEP, :, :, :, 1 - c], in_core.at[j % SLOTS], sc.at[j % SLOTS], rc.at[j % SLOTS], core_peer)

    def one_copies(j):
        p, s = j % DEEP, j % SLOTS
        return (remote(part.at[p, :, :, 1 - x, c, :, low], in_one_a.at[s], s1a.at[s], r1a.at[s], x_peer),
                remote(part.at[p, :, 1 - y, :, c, :, high], in_one_b.at[s], s1b.at[s], r1b.at[s], y_peer))

    def two_copies(j):
        p, s = j % DEEP, j % SLOTS
        return (remote(part.at[p, :, 1 - y, x, c, :, low], in_two_a.at[s], s2a.at[s], r2a.at[s], y_peer),
                remote(part.at[p, :, y, 1 - x, c, :, high], in_two_b.at[s], s2b.at[s], r2b.at[s], x_peer))

    def line_copies(j):
        p, s = j % DEEP, j % SLOTS
        return [remote(part.at[p, w, y, x, c], in_line.at[s, d], s3.at[d, s], r3.at[d, s], line_peers[d])
                for d, w in enumerate(line)]

    def during(t, lag):
        return pl.when(jnp.logical_and(t >= lag, t < length + lag))

    def stream_step(t):
        @during(t, 4)
        def _():
            j = t - 4
            p, s = j % DEEP, j % SLOTS
            for copy in line_copies(j):
                copy.wait()
            consume(j, (part[p, z, y, x, c] + in_line[s, 0]) + (in_line[s, 1] + in_line[s, 2]))

            @pl.when(j < length - SLOTS)
            def _():
                for d in range(3):
                    signal(free_line.at[d], line_sources[d])

        @during(t, 3)
        def _():
            j = t - 3
            p, s = j % DEEP, j % SLOTS
            for copy in two_copies(j):
                copy.wait()
            for w in range(4):
                part[p, w, y, x, c, :, low] += in_two_a[s, w]
                part[p, w, y, x, c, :, high] += in_two_b[s, w]

            @pl.when(j < length - SLOTS)
            def _():
                signal(free_2a, y_peer)
                signal(free_2b, x_peer)

            @pl.when(j >= SLOTS)
            def _():
                for d in range(3):
                    pl.semaphore_wait(free_line.at[d], 1)

            for copy in line_copies(j):
                copy.start()

        @during(t, 2)
        def _():
            j = t - 2
            p, s = j % DEEP, j % SLOTS
            for copy in one_copies(j):
                copy.wait()
            for w in range(4):
                for v in range(2):
                    part[p, w, v, x, c, :, low] += in_one_a[s, w, v]
                    part[p, w, y, v, c, :, high] += in_one_b[s, w, v]

            @pl.when(j < length - SLOTS)
            def _():
                signal(free_1a, x_peer)
                signal(free_1b, y_peer)

            @pl.when(j >= SLOTS)
            def _():
                pl.semaphore_wait(free_2a, 1)
                pl.semaphore_wait(free_2b, 1)

            for copy in two_copies(j):
                copy.start()

        @during(t, 1)
        def _():
            j = t - 1
            p, s = j % DEEP, j % SLOTS
            core_copy(j).wait()
            for w in range(4):
                for v in range(2):
                    for u in range(2):
                        part[p, w, v, u, c] += in_core[s, w, v, u]

            @pl.when(j < length - SLOTS)
            def _():
                signal(free_core, core_peer)

            @pl.when(j >= SLOTS)
            def _():
                pl.semaphore_wait(free_1a, 1)
                pl.semaphore_wait(free_1b, 1)

            for copy in one_copies(j):
                copy.start()

        @pl.when(t < length)
        def _():
            produce(t, part.at[t % DEEP])

            @pl.when(t >= SLOTS)
            def _():
                pl.semaphore_wait(free_core, 1)

            core_copy(t).start()

    return stream_step


def exchange_scratch(count, rows, features):
    dma, f32 = pltpu.SemaphoreType.DMA, jnp.float32
    return [pltpu.VMEM((rows, features), f32), pltpu.VMEM((count, 7, rows, CHUNK), f32), pltpu.VMEM((rows, CHUNK), f32),
            pltpu.VMEM((count, 4, rows, CHUNK), f32), pltpu.VMEM((rows, CHUNK), f32), pltpu.VMEM((count, rows, features), f32),
            dma((7,)), dma((count, 7)), dma((3,)), dma((count, 3)), dma((7,)), dma((count, 7))]


EXCHANGE_REFS = 12


def exchange_of(spot, refs):
    part_sums, in_plane, own, in_rank, total, sums, send_a, recv_a, send_b, recv_b, send_c, recv_c = refs
    z, y, x, c = spot
    q = (y * 2 + x) * 2 + c
    plane = [(q + d) % 8 for d in range(1, 8)]
    line_peers = peers_of(spot)[4]

    def first_copies(k):
        return [remote(part_sums.at[:, both(p)], in_plane.at[k, d], send_a.at[d], recv_a.at[k, d], z * 8 + p)
                for d, p in enumerate(plane)]

    def second_copies(k):
        return [remote(own, in_rank.at[k, z], send_b.at[d], recv_b.at[k, d], line_peers[d]) for d in range(3)]

    def third_copies(k):
        return [remote(total, sums.at[k, :, both(q)], send_c.at[d], recv_c.at[k, d], z * 8 + p)
                for d, p in enumerate(plane)]

    def begin(k):
        for copy in first_copies(k):
            copy.start()

    def cross(k):
        acc = part_sums[:, both(q)]
        for d, copy in enumerate(first_copies(k)):
            copy.wait()
            acc = acc + in_plane[k, d]
        own[...] = acc
        in_rank[k, z] = acc
        for copy in second_copies(k):
            copy.start()

    def spread(k):
        for copy in second_copies(k):
            copy.wait()
        acc = (in_rank[k, 0] + in_rank[k, 1]) + (in_rank[k, 2] + in_rank[k, 3])
        total[...] = acc
        sums[k, :, both(q)] = acc
        for copy in third_copies(k):
            copy.start()

    def finish(k):
        for copy in third_copies(k):
            copy.wait()

    return begin, cross, spread, finish


def everyone(spot):
    z, y, x, c = spot
    q = (y * 2 + x) * 2 + c
    return [z * 8 + (q + d) % 8 for d in range(1, 8)] + peers_of(spot)[4]


def looped(count, body):
    def run(j, carry):
        body(j)
        return carry
    lax.fori_loop(0, count, run, 0)


def ascent_kernel(feat_ref, w_one_ref, w_two_ref, w_three_ref, aux_ref,
                  hat_one_ref, hat_two_ref, hat_three_ref, act_one_ref, act_two_ref, embed_ref, inv_ref,
                  weights, hats, acts, load_two, load_three, save_hat, save_act, *refs):
    me, *spot = coords()
    begin, cross, spread, finish = exchange_of(spot, refs)
    part_sums, sums = refs[0], refs[5]
    side = feat_ref.shape[0] // 2
    count = side * 32
    chunks = aux_ref.shape[1] // CHUNK
    load = [pltpu.make_async_copy(w_two_ref, weights.at[0], load_two),
            pltpu.make_async_copy(w_three_ref, weights.at[1], load_three)]
    for copy in load:
        copy.start()
    save_hats = [pltpu.make_async_copy(hats.at[k % 2], ref, save_hat.at[k])
                 for k, ref in enumerate((hat_one_ref, hat_two_ref, hat_three_ref))]
    save_acts = [pltpu.make_async_copy(acts.at[k % 2], ref, save_act.at[k])
                 for k, ref in enumerate((act_one_ref, act_two_ref, embed_ref))]
    for layer in range(3):
        if layer:
            load[layer - 1].wait()
        if layer == 2:
            save_hats[0].wait()
            save_acts[0].wait()
        source = feat_ref if layer == 0 else acts.at[layer - 1]
        weight = w_one_ref if layer == 0 else weights.at[layer - 1]
        hat_ref, act_ref = hats.at[layer % 2], acts.at[layer % 2]

        def product(j):
            cols = both(j)
            for view in range(2):
                span = slice(view * side, (view + 1) * side)
                value = jnp.dot(source[span, :], weight[:, cols], preferred_element_type=jnp.float32)
                hat_ref[span, cols] = value
                part_sums[view:view + 1, cols] = jnp.sum(value, axis=0, keepdims=True)
                part_sums[2 + view:3 + view, cols] = jnp.sum(value * value, axis=0, keepdims=True)

        def normalise(j):
            cols = both(j)
            for view in range(2):
                span = slice(view * side, (view + 1) * side)
                mean = sums[layer, view:view + 1, cols] / count
                inv = lax.rsqrt(sums[layer, 2 + view:3 + view, cols] / count - mean * mean + NORM_EPS)
                inv_ref[2 * layer + view:2 * layer + view + 1, cols] = inv
                hat = (hat_ref[span, cols] - mean) * inv
                hat_ref[span, cols] = hat
                if layer < 2:
                    gain, shift = aux_ref[2 * layer:2 * layer + 1, cols], aux_ref[2 * layer + 1:2 * layer + 2, cols]
                    hat = jnp.maximum(gain * hat + shift, 0.0)
                act_ref[span, cols] = hat.astype(jnp.bfloat16)

        looped(chunks, product)
        if layer == 0:
            greet(everyone(spot))
        begin(layer)
        cross(layer)
        spread(layer)
        finish(layer)
        looped(chunks, normalise)
        save_hats[layer].start()
        save_acts[layer].start()
    for k in (1, 2):
        save_hats[k].wait()
        save_acts[k].wait()


def ascend(feat, w_one, w_two, w_three, aux, collective_id):
    depth, features = feat.shape[0], w_two.shape[0]
    dma, f32, bf16 = pltpu.SemaphoreType.DMA, jnp.float32, jnp.bfloat16
    away = pl.BlockSpec(memory_space=pltpu.HBM)
    wide, narrow = jax.ShapeDtypeStruct((depth, features), f32), jax.ShapeDtypeStruct((depth, features), bf16)
    return pl.pallas_call(
        ascent_kernel,
        out_shape=(wide, wide, wide, narrow, narrow, narrow, jax.ShapeDtypeStruct((6, features), f32)),
        in_specs=[VMEM, VMEM, away, away, VMEM], out_specs=(away,) * 6 + (VMEM,),
        scratch_shapes=[pltpu.VMEM((2, features, features), bf16), pltpu.VMEM((2, depth, features), f32),
                        pltpu.VMEM((2, depth, features), bf16), dma, dma, dma((3,)), dma((3,))]
                       + exchange_scratch(3, 4, features),
        compiler_params=params(collective_id),
        name="ascend",
    )(feat, w_one, w_two, w_three, aux)


def corr_kernel(embed_ref, hat_ref, inv_ref, lam_ref, top_ref, loss_ref,
                grads, hats, mine, whole, load_hat, t3, u3, t2a, u2a, t2b, u2b, t1a, u1a, t1b, u1b, tc, uc, *refs):
    me, *spot = coords()
    z, y, x, c = spot
    core_peer, x_peer, y_peer, line, line_peers = peers_of(spot)
    stream_refs, exchange_refs = refs[:STREAM_REFS], refs[STREAM_REFS:]
    begin, cross, spread, finish = exchange_of(spot, exchange_refs)
    part_sums, sums = exchange_refs[0], exchange_refs[5]
    side, features = embed_ref.shape[0] // 2, embed_ref.shape[1]
    count = side * 32
    chunks = features // CHUNK
    first, second = slice(0, side), slice(side, 2 * side)
    load = pltpu.make_async_copy(hat_ref, hats, load_hat)
    load.start()
    grads[first, :] = jnp.zeros((side, features), jnp.float32)
    greet(everyone(spot))

    def half_a(j):
        return pl.ds(pl.multiple_of(j * CHUNK, HALF), HALF)

    def half_b(j):
        return pl.ds(pl.multiple_of(j * CHUNK + HALF, HALF), HALF)

    def line_copies(j):
        return [remote(mine.at[:, both(j)], whole.at[z, y, x, c, :, both(j)],
                       t3.at[d, j], u3.at[d, j], line_peers[d]) for d in range(3)]

    def two_copies(j):
        a, b = whole.at[:, y, x, c, :, half_a(j)], whole.at[:, y, x, c, :, half_b(j)]
        return (remote(a, a, t2a.at[j], u2a.at[j], y_peer), remote(b, b, t2b.at[j], u2b.at[j], x_peer))

    def one_copies(j):
        a, b = whole.at[:, :, x, c, :, half_a(j)], whole.at[:, y, :, c, :, half_b(j)]
        return (remote(a, a, t1a.at[j], u1a.at[j], x_peer), remote(b, b, t1b.at[j], u1b.at[j], y_peer))

    def core_copy(j):
        a = whole.at[:, :, :, c, :, both(j)]
        return remote(a, a, tc.at[j], uc.at[j], core_peer)

    def produce(j, slot):
        rhs = embed_ref[second, both(j)]

        def tile(w):
            product = lax.dot_general(embed_ref[first, pl.ds(pl.multiple_of(w * 512, 512), 512)], rhs, FIRST_DIMS,
                                      preferred_element_type=jnp.float32)
            slot[w] = product.reshape(2, 2, 2, BLOCK, CHUNK)

        looped(4, tile)

    def consume(j, block):
        corr = block / count
        lam = lam_ref[0:1, 0:1]
        row = me * BLOCK + lax.broadcasted_iota(jnp.int32, corr.shape, 0)
        col = j * CHUNK + lax.broadcasted_iota(jnp.int32, corr.shape, 1)
        gap = 1.0 - corr
        part_sums[4:5, both(j)] = jnp.sum(jnp.where(row == col, gap * gap, lam * corr * corr), axis=0, keepdims=True)
        grad = (jnp.where(row == col, -2.0 * gap, 2.0 * lam * corr) / count).astype(jnp.bfloat16)
        mine[:, both(j)] = grad
        whole[z, y, x, c, :, both(j)] = grad
        for copy in line_copies(j):
            copy.start()

    stream_step = stream_of(chunks, spot, stream_refs, produce, consume)

    def during(t, lag):
        return pl.when(jnp.logical_and(t >= lag, t < chunks + lag))

    def step(t):
        @during(t, 7)
        def _():
            for copy in one_copies(t - 7):
                copy.wait()
            core_copy(t - 7).start()

        @during(t, 6)
        def _():
            for copy in two_copies(t - 6):
                copy.wait()
            for copy in one_copies(t - 6):
                copy.start()

        @during(t, 5)
        def _():
            for copy in line_copies(t - 5):
                copy.wait()
            for copy in two_copies(t - 5):
                copy.start()

        stream_step(t)

        @during(t, 8)
        def _():
            j = t - 8
            core_copy(j).wait()
            slab = whole[:, :, :, :, :, both(j)].reshape(features, CHUNK)
            grads[second, both(j)] = jnp.dot(embed_ref[first, :], slab, preferred_element_type=jnp.float32)
            grads[first, :] += lax.dot_general(embed_ref[second, both(j)], slab, (((1,), (1,)), ((), ())),
                                               preferred_element_type=jnp.float32)

    looped(chunks + 8, step)
    load.wait()

    def add_up(j):
        cols = both(j)
        for view in range(2):
            span = slice(view * side, (view + 1) * side)
            grad = grads[span, cols]
            part_sums[view:view + 1, cols] = jnp.sum(grad, axis=0, keepdims=True)
            part_sums[2 + view:3 + view, cols] = jnp.sum(grad * hats[span, cols], axis=0, keepdims=True)

    looped(chunks, add_up)
    begin(0)
    cross(0)
    spread(0)
    finish(0)
    loss_ref[...] = sums[0, 4:5, :]

    def normalise(j):
        cols = both(j)
        for view in range(2):
            span = slice(view * side, (view + 1) * side)
            sum_one = sums[0, view:view + 1, cols] / count
            sum_two = sums[0, 2 + view:3 + view, cols] / count
            grad = inv_ref[view:view + 1, cols] * (grads[span, cols] - (sum_one + hats[span, cols] * sum_two))
            top_ref[span, cols] = grad.astype(jnp.bfloat16)

    looped(chunks, normalise)


def correlate(embed, hat, inv, lam, collective_id):
    depth, features = embed.shape
    chunks = features // CHUNK
    dma, f32, bf16 = pltpu.SemaphoreType.DMA, jnp.float32, jnp.bfloat16
    return pl.pallas_call(
        corr_kernel,
        out_shape=(jax.ShapeDtypeStruct((depth, features), bf16), jax.ShapeDtypeStruct((1, features), f32)),
        in_specs=[VMEM, pl.BlockSpec(memory_space=pltpu.HBM), VMEM, VMEM], out_specs=(VMEM, VMEM),
        scratch_shapes=[pltpu.VMEM((depth, features), f32), pltpu.VMEM((depth, features), f32),
                        pltpu.VMEM((BLOCK, features), bf16), pltpu.VMEM((4, 2, 2, 2, BLOCK, features), bf16), dma]
                       + [dma((3, chunks))] * 2 + [dma((chunks,))] * 10
                       + stream_scratch() + exchange_scratch(1, 5, features),
        compiler_params=params(collective_id),
        name="correlate",
    )(embed, hat, inv, lam)


def descent_kernel(top_ref, act_two_ref, act_one_ref, feat_ref, w_three_ref, w_two_ref, normed_two_ref, normed_one_ref, aux_ref,
                   outs_ref, sums_ref,
                   rows, acts, weights, normed, masked, load_rows, load_acts, load_weights, load_normed, *refs):
    me, *spot = coords()
    exchange_refs = refs[STREAM_REFS:]
    begin, cross, spread, finish = exchange_of(spot, exchange_refs)
    part_sums, sums = exchange_refs[0], exchange_refs[5]
    side = rows.shape[1] // 2
    count = side * 32

    copy_rows = pltpu.make_async_copy(top_ref, rows.at[0], load_rows)
    copy_act_two = pltpu.make_async_copy(act_two_ref, acts, load_acts)
    copy_act_one = pltpu.make_async_copy(act_one_ref, acts, load_acts)
    copy_w_three = pltpu.make_async_copy(w_three_ref, weights, load_weights)
    copy_w_two = pltpu.make_async_copy(w_two_ref, weights, load_weights)
    copy_normed_two = pltpu.make_async_copy(normed_two_ref, normed, load_normed)
    copy_normed_one = pltpu.make_async_copy(normed_one_ref, normed, load_normed)
    for copy in (copy_rows, copy_act_two, copy_w_three, copy_normed_two):
        copy.start()
    greet(everyone(spot))
    copy_rows.wait()

    def produce(t, slot):
        @pl.when(t < 16)
        def _():
            rhs = rows[t // 8, :, both(t % 8)]

            def tile(w):
                product = lax.dot_general(acts[:, pl.ds(pl.multiple_of(w * 512, 512), 512)], rhs, FIRST_DIMS,
                                          preferred_element_type=jnp.float32)
                slot[w] = product.reshape(2, 2, 2, BLOCK, CHUNK)

            looped(4, tile)

        @pl.when(t >= 16)
        def _():
            for k in range(4):
                product = jnp.dot(feat_ref[...], rows[2, :, both((t - 16) * 4 + k)], preferred_element_type=jnp.float32)
                slot[:, :, :, :, 16 * k:16 * k + 16, :] = product.reshape(4, 2, 2, 2, 16, CHUNK)

    def consume(j, block):
        outs_ref[j] = block

    stream_step = stream_of(STREAM, spot, refs[:STREAM_REFS], produce, consume)

    def pull(layer, j):
        cols = both(j)
        gain, shift = aux_ref[layer, 0:1, cols], aux_ref[layer, 1:2, cols]
        weight = weights[cols, :]
        for view in range(2):
            span = slice(view * side, (view + 1) * side)
            grad = lax.dot_general(rows[layer, span, :], weight, (((1,), (1,)), ((), ())),
                                   preferred_element_type=jnp.float32)
            hat = normed[span, cols]
            grad = jnp.where(gain * hat + shift > 0, grad, 0.0)
            masked[span, cols] = grad
            part_sums[view:view + 1, cols] = jnp.sum(grad, axis=0, keepdims=True)
            part_sums[2 + view:3 + view, cols] = jnp.sum(grad * hat, axis=0, keepdims=True)

    def push(layer, j):
        cols = both(j)
        gain = aux_ref[layer, 0:1, cols]
        for view in range(2):
            span = slice(view * side, (view + 1) * side)
            inv = aux_ref[layer, 2 + view:3 + view, cols]
            sum_one = sums[layer, view:view + 1, cols] / count
            sum_two = sums[layer, 2 + view:3 + view, cols] / count
            grad = inv * (masked[span, cols] - (sum_one + normed[span, cols] * sum_two))
            rows[layer + 1, span, cols] = (gain * grad).astype(jnp.bfloat16)

    def descend_step(t):
        layer, phase = t // 8, t % 8

        def at(k):
            return pl.when(jnp.logical_and(t < 16, phase == k))

        def pulls(lo, hi):
            def body(j, carry):
                pull(layer, j)
                return carry
            lax.fori_loop(lo, hi, body, 0)

        def pushes(lo, hi):
            def body(j, carry):
                push(layer, j)
                return carry
            lax.fori_loop(lo, hi, body, 0)

        @at(1)
        def _():
            copy_w_three.wait()
            copy_normed_two.wait()
            pulls(0, 2)

        @at(2)
        def _():
            pulls(2, 5)

        @at(3)
        def _():
            pulls(5, 8)
            begin(layer)

        @pl.when(t == 3)
        def _():
            copy_w_two.start()

        @at(4)
        def _():
            cross(layer)

        @at(5)
        def _():
            spread(layer)

        @at(6)
        def _():
            finish(layer)
            pushes(0, 4)

        @at(7)
        def _():
            pushes(4, 8)

        @pl.when(t == 7)
        def _():
            copy_act_one.start()
            copy_normed_one.start()

    def step(t, carry):
        @pl.when(t == 0)
        def _():
            copy_act_two.wait()

        @pl.when(t == 8)
        def _():
            copy_act_one.wait()

        stream_step(t)
        descend_step(t)
        return carry

    lax.fori_loop(0, STREAM + 4, step, 0)
    sums_ref[...] = sums[...]


def descend(top, act_two, act_one, feat_t, w_three, w_two, normed_two, normed_one, aux, collective_id):
    depth, features = top.shape
    dma, f32, bf16 = pltpu.SemaphoreType.DMA, jnp.float32, jnp.bfloat16
    away = pl.BlockSpec(memory_space=pltpu.HBM)
    return pl.pallas_call(
        descent_kernel,
        out_shape=(jax.ShapeDtypeStruct((STREAM, BLOCK, CHUNK), f32), jax.ShapeDtypeStruct((2, 4, features), f32)),
        in_specs=[away, away, away, VMEM, away, away, away, away, VMEM], out_specs=(VMEM, VMEM),
        scratch_shapes=[pltpu.VMEM((3, depth, features), bf16), pltpu.VMEM((depth, features), bf16),
                        pltpu.VMEM((features, features), bf16), pltpu.VMEM((depth, features), f32),
                        pltpu.VMEM((depth, features), f32),
                        ] + [dma] * 4 + stream_scratch() + exchange_scratch(2, 4, features),
        compiler_params=params(collective_id),
        name="descend",
    )(top, act_two, act_one, feat_t, w_three, w_two, normed_two, normed_one, aux)


def solution(mesh):
    shards = mesh.shape[AXIS]

    def local_step(h_a, h_b, w_one, w_two, w_three, gain_one, shift_one, gain_two, shift_two, lam_off):
        rows_dev = h_a.shape[0]
        features = w_two.shape[0]
        block_rows = features // shards
        feat_rows = jnp.concatenate([h_a, h_b], axis=0)
        in_rows = feat_rows.shape[1] // shards
        feat_t = jnp.pad(feat_rows.T.reshape(shards, in_rows, 2 * rows_dev), ((0, 0), (0, 16 - in_rows), (0, 0)))
        feat_t = feat_t.reshape(shards * 16, 2 * rows_dev)
        hat_one, hat_two, hat_out, act_one, act_two, embed, inv = ascend(
            feat_rows, w_one, w_two, w_three, jnp.stack([gain_one, shift_one, gain_two, shift_two]), 0)
        top, loss_row = correlate(embed, hat_out, inv[4:], jnp.full((1, 128), lam_off), 1)
        aux = jnp.stack([jnp.stack([gain_two, shift_two, inv[2], inv[3]]), jnp.stack([gain_one, shift_one, inv[0], inv[1]])])
        outs, sums = descend(top, act_two, act_one, feat_t, w_three, w_two, hat_two, hat_one, aux, 2)

        def block_of(chunk):
            return chunk.transpose(1, 0, 2).reshape(block_rows, features)

        grad_w_one = outs[16:].reshape(2, 4, 16, CHUNK).transpose(2, 0, 1, 3).reshape(16, features)[:in_rows]
        return (jnp.sum(loss_row), grad_w_one, block_of(outs[8:16]), block_of(outs[:8]),
                sums[1, 2] + sums[1, 3], sums[1, 0] + sums[1, 1], sums[0, 2] + sums[0, 3], sums[0, 0] + sums[0, 1])

    row_spec = P(AXIS, None)
    whole_mat = P(None, None)
    whole_vec = P(None)
    return jax.shard_map(
        local_step, mesh=mesh,
        in_specs=(row_spec, row_spec, whole_mat, whole_mat, whole_mat,
                  whole_vec, whole_vec, whole_vec, whole_vec, P()),
        out_specs=(P(), row_spec, row_spec, row_spec, whole_vec, whole_vec, whole_vec, whole_vec),
        check_vma=False)
```

time: 994 us -> 422 us (0.42); the launches traced: 979 us -> 421 us
  waiting for transfers between devices: 407 us -> 0 us
  Pallas kernels: 0 us -> 403 us
  blocking collectives: 339 us -> 0 us
  matrix products: 134 us -> 0 us
  other arithmetic: 40.8 us -> 4.08 us
  starting transfers between devices: 28.2 us -> 0 us
  between operations: 15.3 us -> 1.43 us
    pallas_call x0 -> x3, Pallas kernels: none -> 403 us  [the longest x1 190 us: descend(): pl.pallas_call(descent_kernel, out_shape=(jax.ShapeDtypeStruct((STREAM, B...]
    psum x1 -> x0, waiting for transfers between devices: 277 us -> none  [local_step(): corr_mat = lax.psum(corr_part, 'data') / total_rows]
    psum x6 -> x0, blocking collectives: 250 us -> none  [the longest x3 127 us: norm_backward(): lax.psum(jnp.stack([jnp.sum(grad_out, axis=1), jnp.sum(grad_out * normed,...]
    dot_general x11 -> x0, matrix products: 134 us -> none  [the longest x1 16.9 us: local_step(): lax.dot_general(grad_hidden_two, w_two, LAST_DIMS, preferred_element_type...]
    reduce_scatter x2 -> x0, waiting for transfers between devices: 123 us -> none  [the longest x1 123 us: local_step(): lax.psum_scatter(lax.dot_general(act_one, grad_hidden_two, ROW_DIMS, pref...]
    unnamed x1 -> x0, blocking collectives: 89.4 us -> none
    unnamed x8 -> x0, starting transfers between devices: 28.1 us -> none
    convert_element_type x4 -> x0, other arithmetic: 25.9 us -> none  [the longest x1 7.15 us: local_step(): (gain_one * grad_hidden_one).astype(jnp.bfloat16).reshape(2 * rows_dev, -1)]
  transfers between devices with their start and end apart: 11 -> 0, of which waited for: 3 -> 0; matrix products, arithmetic and copies ran while one was open for 17% -> 0% of each run, Pallas kernels for 0% -> 0%
where the time goes in v3:
time: 422 us; the launch traced here: 421 us
  Pallas kernels  403 us (95%)
  local copies, waits for them, and re-layouts  13.1 us (3%)
    pallas_call x1, Pallas kernels, descend(): pl.pallas_call(descent_kernel, out_shape=(jax.ShapeDtypeStruct((STREAM, B...  190 us
    pallas_call x1, Pallas kernels, correlate(): pl.pallas_call(corr_kernel, out_shape=(jax.ShapeDtypeStruct((depth, featu...  141 us
    pallas_call x1, Pallas kernels, ascend(): pl.pallas_call(ascent_kernel, out_shape=(wide, wide, wide, narrow, narrow...  72 us

profile of v3, /device:TPU:0, one launch (start us, length us, event | category | flops | bytes accessed | tf_op | source)
XLA Modules:
  0.0 421.4 jit_solution(14814161818717049625)
XLA Ops:
  0.6 1.8 constant_dynamic-update-slice_fusion.1
  2.4 1.8 constant_dynamic-update-slice_fusion.feat_ref
  4.2 1.4 pad_maximum_fusion.1.aux_ref
  5.6 72.0 %ascend.1 = (f32[1024,2048]{1,0:T(8,128)}, f32[1024,2048]{1,0:T(8,128)}, f32[1024,2048]{1,0:T(8,128)}, bf16[1024,2048]{1,0:T(8,128)(2,1)}, bf16[1024,2048]{1,0:T...) custom-call(bf16[1024,384]{1,0:T(8,128)(2,1)} %constant_dynamic-update-slice_fusion.feat_ref, ...), custom_call_target="tpu_custom_call" | custom-call | tf_op jit(solution)/shard_map/ascend/pallas_call | solution.py:340
  77.6 1.6 fusion
  79.8 0.5 broadcast_in_dim.3.lam_ref
  80.4 141.0 %correlate.1 = (bf16[1024,2048]{1,0:T(8,128)(2,1)}, f32[1,2048]{1,0:T(1,128)}) custom-call(bf16[1024,2048]{1,0:T(8,128)(2,1)} %get-tuple-element.19.embed_ref, f32[1024,2048]{1,0:T(8,128)} %get-tuple-element.20.hat_ref, f32[2,2048]{1,0:T(2,128)} %get-tuple-element.38.inv_ref, f32[1,128]{1,0:T(1,128)} %broadcast_in_dim.3.lam_ref), custom_call_target="tpu_custom_call" | custom-call | tf_op jit(solution)/shard_map/correlate/pallas_call | solution.py:485
  221.4 0.0 copy-start.1
  221.4 0.0 copy-start.2
  221.4 0.0 copy-start.5
  221.4 1.3 reduce_sum.9
  222.8 1.4 copy.20
  224.2 0.2 reshape.37
  224.4 1.1 pad.4
  225.6 0.1 maximum_bitcast_fusion
  225.6 0.6 pad_maximum_fusion.aux_ref
  226.3 189.8 %descend.1 = (f32[18,64,256]{2,1,0:T(8,128)}, f32[2,4,2048]{2,1,0:T(4,128)}) custom-call(bf16[1024,2048]{1,0:T(8,128)(2,1)} %get-tuple-element.23.top_ref, bf16[1024,2048]{1,0:T(8,128)(2,1)} %get-tuple-element.24.act_two_ref, bf16[1024,2048]{1,0:T(8,128)(2,1)} %get-tuple-element.25.act_one_ref, bf16[512,1024]{1,0:T(8,128)(2,1)} %bitcast.26, ...), custom_call_target="tpu_custom_call" | custom-call | tf_op jit(solution)/shard_map/descend/pallas_call | solution.py:648
  416.0 0.9 slice.55
  417.0 0.1 copy.21
  417.1 0.7 slice.57
  417.8 1.3 slice_bitcast_fusion
  419.1 0.8 copy.24
  419.9 0.8 copy.25
  420.8 0.6 slice_add_fusion
  (11 shorter events, 0.0 us)
Async XLA Ops:
  221.4 4.2 copy-start.1
  221.4 4.1 copy-start.2
  221.4 4.1 copy-start.3
  221.4 4.1 copy-start.4
  221.4 4.1 copy-start.5
  221.4 4.1 copy-start.6
  416.0 4.7 %copy-start = (f32[2,4,2048]{2,1,0:T(4,128)S(1)}, f32[2,4,2048]{2,1,0:T(4,128)}, u32[]{:S(2)}) copy-start(f32[2,4,2048]{2,1,0:T(4,128)} %get-tuple-element.29) | copy-start | bytes 196612

commit v4 on v3

--- a/solution.py
+++ b/solution.py
@@ -101,40 +101,26 @@
         return pl.when(jnp.logical_and(t >= lag, t < length + lag))
 
     def stream_step(t):
-        @during(t, 4)
-        def _():
-            j = t - 4
+        @during(t, 1)
+        def _():
+            j = t - 1
             p, s = j % DEEP, j % SLOTS
-            for copy in line_copies(j):
-                copy.wait()
-            consume(j, (part[p, z, y, x, c] + in_line[s, 0]) + (in_line[s, 1] + in_line[s, 2]))
+            core_copy(j).wait()
+            for w in range(4):
+                for v in range(2):
+                    for u in range(2):
+                        part[p, w, v, u, c] += in_core[s, w, v, u]
 
             @pl.when(j < length - SLOTS)
             def _():
-                for d in range(3):
-                    signal(free_line.at[d], line_sources[d])
-
-        @during(t, 3)
-        def _():
-            j = t - 3
-            p, s = j % DEEP, j % SLOTS
-            for copy in two_copies(j):
-                copy.wait()
-            for w in range(4):
-                part[p, w, y, x, c, :, low] += in_two_a[s, w]
-                part[p, w, y, x, c, :, high] += in_two_b[s, w]
-
-            @pl.when(j < length - SLOTS)
-            def _():
-                signal(free_2a, y_peer)
-                signal(free_2b, x_peer)
+                signal(free_core, core_peer)
 
             @pl.when(j >= SLOTS)
             def _():
-                for d in range(3):
-                    pl.semaphore_wait(free_line.at[d], 1)
-
-            for copy in line_copies(j):
+                pl.semaphore_wait(free_1a, 1)
+                pl.semaphore_wait(free_1b, 1)
+
+            for copy in one_copies(j):
                 copy.start()
 
         @during(t, 2)
@@ -161,27 +147,41 @@
             for copy in two_copies(j):
                 copy.start()
 
-        @during(t, 1)
-        def _():
-            j = t - 1
+        @during(t, 3)
+        def _():
+            j = t - 3
             p, s = j % DEEP, j % SLOTS
-            core_copy(j).wait()
+            for copy in two_copies(j):
+                copy.wait()
             for w in range(4):
-                for v in range(2):
-                    for u in range(2):
-                        part[p, w, v, u, c] += in_core[s, w, v, u]
+                part[p, w, y, x, c, :, low] += in_two_a[s, w]
+                part[p, w, y, x, c, :, high] += in_two_b[s, w]
 
             @pl.when(j < length - SLOTS)
             def _():
-                signal(free_core, core_peer)
+                signal(free_2a, y_peer)
+                signal(free_2b, x_peer)
 
             @pl.when(j >= SLOTS)
             def _():
-                pl.semaphore_wait(free_1a, 1)
-                pl.semaphore_wait(free_1b, 1)
-
-            for copy in one_copies(j):
+                for d in range(3):
+                    pl.semaphore_wait(free_line.at[d], 1)
+
+            for copy in line_copies(j):
                 copy.start()
+
+        @during(t, 4)
+        def _():
+            j = t - 4
+            p, s = j % DEEP, j % SLOTS
+            for copy in line_copies(j):
+                copy.wait()
+            consume(j, (part[p, z, y, x, c] + in_line[s, 0]) + (in_line[s, 1] + in_line[s, 2]))
+
+            @pl.when(j < length - SLOTS)
+            def _():
+                for d in range(3):
+                    signal(free_line.at[d], line_sources[d])
 
         @pl.when(t < length)
         def _():
@@ -267,15 +267,15 @@
     lax.fori_loop(0, count, run, 0)
 
 
-def ascent_kernel(feat_ref, w_one_ref, w_two_ref, w_three_ref, aux_ref,
+def ascent_kernel(view_a_ref, view_b_ref, w_one_ref, w_two_ref, w_three_ref, aux_ref,
                   hat_one_ref, hat_two_ref, hat_three_ref, act_one_ref, act_two_ref, embed_ref, inv_ref,
                   weights, hats, acts, load_two, load_three, save_hat, save_act, *refs):
     me, *spot = coords()
     begin, cross, spread, finish = exchange_of(spot, refs)
     part_sums, sums = refs[0], refs[5]
-    side = feat_ref.shape[0] // 2
+    side = view_a_ref.shape[0]
     count = side * 32
-    chunks = aux_ref.shape[1] // CHUNK
+    chunks = aux_ref.shape[2] // CHUNK
     load = [pltpu.make_async_copy(w_two_ref, weights.at[0], load_two),
             pltpu.make_async_copy(w_three_ref, weights.at[1], load_three)]
     for copy in load:
@@ -290,7 +290,6 @@
         if layer == 2:
             save_hats[0].wait()
             save_acts[0].wait()
-        source = feat_ref if layer == 0 else acts.at[layer - 1]
         weight = w_one_ref if layer == 0 else weights.at[layer - 1]
         hat_ref, act_ref = hats.at[layer % 2], acts.at[layer % 2]
 
@@ -298,7 +297,8 @@
             cols = both(j)
             for view in range(2):
                 span = slice(view * side, (view + 1) * side)
-                value = jnp.dot(source[span, :], weight[:, cols], preferred_element_type=jnp.float32)
+                source = (view_a_ref, view_b_ref)[view][...] if layer == 0 else acts[layer - 1, span, :]
+                value = jnp.dot(source, weight[:, cols], preferred_element_type=jnp.float32)
                 hat_ref[span, cols] = value
                 part_sums[view:view + 1, cols] = jnp.sum(value, axis=0, keepdims=True)
                 part_sums[2 + view:3 + view, cols] = jnp.sum(value * value, axis=0, keepdims=True)
@@ -309,11 +309,11 @@
                 span = slice(view * side, (view + 1) * side)
                 mean = sums[layer, view:view + 1, cols] / count
                 inv = lax.rsqrt(sums[layer, 2 + view:3 + view, cols] / count - mean * mean + NORM_EPS)
-                inv_ref[2 * layer + view:2 * layer + view + 1, cols] = inv
+                inv_ref[layer, view:view + 1, cols] = inv
                 hat = (hat_ref[span, cols] - mean) * inv
                 hat_ref[span, cols] = hat
                 if layer < 2:
-                    gain, shift = aux_ref[2 * layer:2 * layer + 1, cols], aux_ref[2 * layer + 1:2 * layer + 2, cols]
+                    gain, shift = aux_ref[layer, 0:1, cols], aux_ref[layer, 1:2, cols]
                     hat = jnp.maximum(gain * hat + shift, 0.0)
                 act_ref[span, cols] = hat.astype(jnp.bfloat16)
 
@@ -332,21 +332,21 @@
         save_acts[k].wait()
 
 
-def ascend(feat, w_one, w_two, w_three, aux, collective_id):
-    depth, features = feat.shape[0], w_two.shape[0]
+def ascend(view_a, view_b, w_one, w_two, w_three, aux, collective_id):
+    depth, features = 2 * view_a.shape[0], w_two.shape[0]
     dma, f32, bf16 = pltpu.SemaphoreType.DMA, jnp.float32, jnp.bfloat16
     away = pl.BlockSpec(memory_space=pltpu.HBM)
     wide, narrow = jax.ShapeDtypeStruct((depth, features), f32), jax.ShapeDtypeStruct((depth, features), bf16)
     return pl.pallas_call(
         ascent_kernel,
-        out_shape=(wide, wide, wide, narrow, narrow, narrow, jax.ShapeDtypeStruct((6, features), f32)),
-        in_specs=[VMEM, VMEM, away, away, VMEM], out_specs=(away,) * 6 + (VMEM,),
+        out_shape=(wide, wide, wide, narrow, narrow, narrow, jax.ShapeDtypeStruct((3, 2, features), f32)),
+        in_specs=[VMEM, VMEM, VMEM, away, away, VMEM], out_specs=(away,) * 6 + (VMEM,),
         scratch_shapes=[pltpu.VMEM((2, features, features), bf16), pltpu.VMEM((2, depth, features), f32),
                         pltpu.VMEM((2, depth, features), bf16), dma, dma, dma((3,)), dma((3,))]
                        + exchange_scratch(3, 4, features),
         compiler_params=params(collective_id),
         name="ascend",
-    )(feat, w_one, w_two, w_three, aux)
+    )(view_a, view_b, w_one, w_two, w_three, aux)
 
 
 def corr_kernel(embed_ref, hat_ref, inv_ref, lam_ref, top_ref, loss_ref,
@@ -417,11 +417,14 @@
         return pl.when(jnp.logical_and(t >= lag, t < chunks + lag))
 
     def step(t):
-        @during(t, 7)
-        def _():
-            for copy in one_copies(t - 7):
+        stream_step(t)
+
+        @during(t, 5)
+        def _():
+            for copy in line_copies(t - 5):
                 copy.wait()
-            core_copy(t - 7).start()
+            for copy in two_copies(t - 5):
+                copy.start()
 
         @during(t, 6)
         def _():
@@ -430,14 +433,11 @@
             for copy in one_copies(t - 6):
                 copy.start()
 
-        @during(t, 5)
-        def _():
-            for copy in line_copies(t - 5):
+        @during(t, 7)
+        def _():
+            for copy in one_copies(t - 7):
                 copy.wait()
-            for copy in two_copies(t - 5):
-                copy.start()
-
-        stream_step(t)
+            core_copy(t - 7).start()
 
         @during(t, 8)
         def _():
@@ -464,7 +464,7 @@
     cross(0)
     spread(0)
     finish(0)
-    loss_ref[...] = sums[0, 4:5, :]
+    loss_ref[...] = jnp.sum(sums[0, 4:5, :], axis=1, keepdims=True)
 
     def normalise(j):
         cols = both(j)
@@ -472,7 +472,7 @@
             span = slice(view * side, (view + 1) * side)
             sum_one = sums[0, view:view + 1, cols] / count
             sum_two = sums[0, 2 + view:3 + view, cols] / count
-            grad = inv_ref[view:view + 1, cols] * (grads[span, cols] - (sum_one + hats[span, cols] * sum_two))
+            grad = inv_ref[2, view:view + 1, cols] * (grads[span, cols] - (sum_one + hats[span, cols] * sum_two))
             top_ref[span, cols] = grad.astype(jnp.bfloat16)
 
     looped(chunks, normalise)
@@ -484,7 +484,7 @@
     dma, f32, bf16 = pltpu.SemaphoreType.DMA, jnp.float32, jnp.bfloat16
     return pl.pallas_call(
         corr_kernel,
-        out_shape=(jax.ShapeDtypeStruct((depth, features), bf16), jax.ShapeDtypeStruct((1, features), f32)),
+        out_shape=(jax.ShapeDtypeStruct((depth, features), bf16), jax.ShapeDtypeStruct((1, 1), f32)),
         in_specs=[VMEM, pl.BlockSpec(memory_space=pltpu.HBM), VMEM, VMEM], out_specs=(VMEM, VMEM),
         scratch_shapes=[pltpu.VMEM((depth, features), f32), pltpu.VMEM((depth, features), f32),
                         pltpu.VMEM((BLOCK, features), bf16), pltpu.VMEM((4, 2, 2, 2, BLOCK, features), bf16), dma]
@@ -495,8 +495,8 @@
     )(embed, hat, inv, lam)
 
 
-def descent_kernel(top_ref, act_two_ref, act_one_ref, feat_ref, w_three_ref, w_two_ref, normed_two_ref, normed_one_ref, aux_ref,
-                   outs_ref, sums_ref,
+def descent_kernel(top_ref, act_two_ref, act_one_ref, feat_ref, w_three_ref, w_two_ref, normed_two_ref, normed_one_ref, aux_ref, inv_ref,
+                   out_three_ref, out_two_ref, out_one_ref, sums_ref,
                    rows, acts, weights, normed, masked, load_rows, load_acts, load_weights, load_normed, *refs):
     me, *spot = coords()
     exchange_refs = refs[STREAM_REFS:]
@@ -536,13 +536,23 @@
                 slot[:, :, :, :, 16 * k:16 * k + 16, :] = product.reshape(4, 2, 2, 2, 16, CHUNK)
 
     def consume(j, block):
-        outs_ref[j] = block
+        @pl.when(j < 8)
+        def _():
+            out_three_ref[:, both(j)] = block
+
+        @pl.when(jnp.logical_and(j >= 8, j < 16))
+        def _():
+            out_two_ref[:, both(j - 8)] = block
+
+        @pl.when(j >= 16)
+        def _():
+            out_one_ref[j - 16] = block
 
     stream_step = stream_of(STREAM, spot, refs[:STREAM_REFS], produce, consume)
 
     def pull(layer, j):
         cols = both(j)
-        gain, shift = aux_ref[layer, 0:1, cols], aux_ref[layer, 1:2, cols]
+        gain, shift = aux_ref[1 - layer, 0:1, cols], aux_ref[1 - layer, 1:2, cols]
         weight = weights[cols, :]
         for view in range(2):
             span = slice(view * side, (view + 1) * side)
@@ -556,10 +566,10 @@
 
     def push(layer, j):
         cols = both(j)
-        gain = aux_ref[layer, 0:1, cols]
+        gain = aux_ref[1 - layer, 0:1, cols]
         for view in range(2):
             span = slice(view * side, (view + 1) * side)
-            inv = aux_ref[layer, 2 + view:3 + view, cols]
+            inv = inv_ref[1 - layer, view:view + 1, cols]
             sum_one = sums[layer, view:view + 1, cols] / count
             sum_two = sums[layer, 2 + view:3 + view, cols] / count
             grad = inv * (masked[span, cols] - (sum_one + normed[span, cols] * sum_two))
@@ -587,37 +597,31 @@
         def _():
             copy_w_three.wait()
             copy_normed_two.wait()
-            pulls(0, 2)
-
-        @at(2)
-        def _():
-            pulls(2, 5)
-
-        @at(3)
-        def _():
-            pulls(5, 8)
+
+        @pl.when(jnp.logical_and(t < 16, jnp.logical_and(phase >= 1, phase <= 4)))
+        def _():
+            pulls(2 * phase - 2, 2 * phase)
+
+        @at(4)
+        def _():
             begin(layer)
 
-        @pl.when(t == 3)
+        @pl.when(t == 4)
         def _():
             copy_w_two.start()
 
-        @at(4)
+        @at(5)
         def _():
             cross(layer)
 
-        @at(5)
-        def _():
-            spread(layer)
-
         @at(6)
         def _():
             finish(layer)
-            pushes(0, 4)
+            pushes(0, 3)
 
         @at(7)
         def _():
-            pushes(4, 8)
+            pushes(3, 8)
 
         @pl.when(t == 7)
         def _():
@@ -632,6 +636,10 @@
         @pl.when(t == 8)
         def _():
             copy_act_one.wait()
+
+        @pl.when(jnp.logical_and(t < 16, t % 8 == 6))
+        def _():
+            spread(t // 8)
 
         stream_step(t)
         descend_step(t)
@@ -641,21 +649,22 @@
     sums_ref[...] = sums[...]
 
 
-def descend(top, act_two, act_one, feat_t, w_three, w_two, normed_two, normed_one, aux, collective_id):
+def descend(top, act_two, act_one, feat_t, w_three, w_two, normed_two, normed_one, aux, inv, collective_id):
     depth, features = top.shape
     dma, f32, bf16 = pltpu.SemaphoreType.DMA, jnp.float32, jnp.bfloat16
     away = pl.BlockSpec(memory_space=pltpu.HBM)
     return pl.pallas_call(
         descent_kernel,
-        out_shape=(jax.ShapeDtypeStruct((STREAM, BLOCK, CHUNK), f32), jax.ShapeDtypeStruct((2, 4, features), f32)),
-        in_specs=[away, away, away, VMEM, away, away, away, away, VMEM], out_specs=(VMEM, VMEM),
+        out_shape=(jax.ShapeDtypeStruct((BLOCK, features), f32), jax.ShapeDtypeStruct((BLOCK, features), f32),
+                   jax.ShapeDtypeStruct((2, BLOCK, CHUNK), f32), jax.ShapeDtypeStruct((2, 4, features), f32)),
+        in_specs=[away, away, away, VMEM, away, away, away, away, VMEM, VMEM], out_specs=(VMEM,) * 4,
         scratch_shapes=[pltpu.VMEM((3, depth, features), bf16), pltpu.VMEM((depth, features), bf16),
                         pltpu.VMEM((features, features), bf16), pltpu.VMEM((depth, features), f32),
                         pltpu.VMEM((depth, features), f32),
                         ] + [dma] * 4 + stream_scratch() + exchange_scratch(2, 4, features),
         compiler_params=params(collective_id),
         name="descend",
-    )(top, act_two, act_one, feat_t, w_three, w_two, normed_two, normed_one, aux)
+    )(top, act_two, act_one, feat_t, w_three, w_two, normed_two, normed_one, aux, inv)
 
 
 def solution(mesh):
@@ -664,22 +673,19 @@
     def local_step(h_a, h_b, w_one, w_two, w_three, gain_one, shift_one, gain_two, shift_two, lam_off):
         rows_dev = h_a.shape[0]
         features = w_two.shape[0]
-        block_rows = features // shards
-        feat_rows = jnp.concatenate([h_a, h_b], axis=0)
-        in_rows = feat_rows.shape[1] // shards
-        feat_t = jnp.pad(feat_rows.T.reshape(shards, in_rows, 2 * rows_dev), ((0, 0), (0, 16 - in_rows), (0, 0)))
-        feat_t = feat_t.reshape(shards * 16, 2 * rows_dev)
-        hat_one, hat_two, hat_out, act_one, act_two, embed, inv = ascend(
-            feat_rows, w_one, w_two, w_three, jnp.stack([gain_one, shift_one, gain_two, shift_two]), 0)
-        top, loss_row = correlate(embed, hat_out, inv[4:], jnp.full((1, 128), lam_off), 1)
-        aux = jnp.stack([jnp.stack([gain_two, shift_two, inv[2], inv[3]]), jnp.stack([gain_one, shift_one, inv[0], inv[1]])])
-        outs, sums = descend(top, act_two, act_one, feat_t, w_three, w_two, hat_two, hat_one, aux, 2)
-
-        def block_of(chunk):
-            return chunk.transpose(1, 0, 2).reshape(block_rows, features)
-
-        grad_w_one = outs[16:].reshape(2, 4, 16, CHUNK).transpose(2, 0, 1, 3).reshape(16, features)[:in_rows]
-        return (jnp.sum(loss_row), grad_w_one, block_of(outs[8:16]), block_of(outs[:8]),
+        in_rows = h_a.shape[1] // shards
+
+        def turned(view):
+            blocks = jnp.pad(view.T.reshape(shards, in_rows, rows_dev), ((0, 0), (0, 16 - in_rows), (0, 0)))
+            return blocks.reshape(shards * 16, rows_dev)
+
+        feat_t = jnp.concatenate([turned(h_a), turned(h_b)], axis=1)
+        aux = jnp.stack([jnp.stack([gain_one, shift_one]), jnp.stack([gain_two, shift_two])])
+        hat_one, hat_two, hat_out, act_one, act_two, embed, inv = ascend(h_a, h_b, w_one, w_two, w_three, aux, 0)
+        top, loss_total = correlate(embed, hat_out, inv, lam_off.reshape(1, 1), 1)
+        out_three, out_two, out_one, sums = descend(top, act_two, act_one, feat_t, w_three, w_two, hat_two, hat_one, aux, inv, 2)
+        grad_w_one = out_one.reshape(2, 4, 16, CHUNK).transpose(2, 0, 1, 3).reshape(16, features)[:in_rows]
+        return (loss_total.reshape(()), grad_w_one, out_two, out_three,
                 sums[1, 2] + sums[1, 3], sums[1, 0] + sums[1, 1], sums[0, 2] + sums[0, 3], sums[0, 0] + sums[0, 1])
 
     row_spec = P(AXIS, None)

time: 422 us -> 404 us (0.957)
  Pallas kernels: 403 us -> 388 us
  local copies, waits for them, and re-layouts: 13.1 us -> 8.04 us
    pallas_call x1, Pallas kernels: 190 us -> 176 us  [descend(): pl.pallas_call(descent_kernel, out_shape=(jax.ShapeDtypeStruct((BLOCK, fe...]
where the time goes in v4:
time: 404 us
  Pallas kernels  388 us (96%)
  local copies, waits for them, and re-layouts  8.04 us (2%)
  other arithmetic  4.2 us (1%)
    pallas_call x1, Pallas kernels, descend(): pl.pallas_call(descent_kernel, out_shape=(jax.ShapeDtypeStruct((BLOCK, fe...  176 us
    pallas_call x1, Pallas kernels, correlate(): pl.pallas_call(corr_kernel, out_shape=(jax.ShapeDtypeStruct((depth, featu...  141 us
    pallas_call x1, Pallas kernels, ascend(): pl.pallas_call(ascent_kernel, out_shape=(wide, wide, wide, narrow, narrow...  72.1 us

profile of v4, /device:TPU:0, one launch (start us, length us, event | category | flops | bytes accessed | tf_op | source)
XLA Modules:
  0.0 403.9 jit_solution(1479624837725186946)
XLA Ops:
  0.6 0.8 maximum_bitcast_fusion
  1.4 0.6 pad_maximum_fusion.1.aux_ref
  2.0 72.1 %ascend.1 = (f32[1024,2048]{1,0:T(8,128)}, f32[1024,2048]{1,0:T(8,128)}, f32[1024,2048]{1,0:T(8,128)}, bf16[1024,2048]{1,0:T(8,128)(2,1)}, bf16[1024,2048]{1,0:T...) custom-call(bf16[512,384]{1,0:T(8,128)(2,1)} %view_a_ref.1, bf16[512,384]{1,0:T(8,128)(2,1)} %view_b_ref.1, ...), custom_call_target="tpu_custom_call" | custom-call | tf_op jit(solution)/shard_map/ascend/pallas_call | solution.py:340
  74.8 140.8 %correlate.1 = (bf16[1024,2048]{1,0:T(8,128)(2,1)}, f32[1,1]{1,0:T(1,128)}) custom-call(bf16[1024,2048]{1,0:T(8,128)(2,1)} %get-tuple-element.21.embed_ref, f32[1024,2048]{1,0:T(8,128)} %get-tuple-element.22.hat_ref, f32[3,2,2048]{2,1,0:T(2,128)} %get-tuple-element.23.inv_ref, f32[1,1]{1,0:T(1,128)} %bitcast.22.lam_ref), custom_call_target="tpu_custom_call" | custom-call | tf_op jit(solution)/shard_map/correlate/pallas_call | solution.py:485
  215.6 1.2 copy.22
  216.8 0.1 reshape.47
  216.9 0.1 pad.8
  216.9 1.2 copy.21
  218.1 0.1 reshape.45
  218.2 0.1 pad.7
  218.3 1.1 pad_maximum_fusion.feat_ref
  219.4 175.6 %descend.1 = (f32[64,2048]{1,0:T(8,128)}, f32[64,2048]{1,0:T(8,128)}, f32[2,64,256]{2,1,0:T(8,128)}, f32[2,4,2048]{2,1,0:T(4,128)}) custom-call(bf16[1024,2048]{1,0:T(8,128)(2,1)} %get-tuple-element.25.top_ref, bf16[1024,2048]{1,0:T(8,128)(2,1)} %get-tuple-element.26.act_two_ref, bf16[1024,2048]{1,0:T(8,128)(2,1)} %get-tuple-element.27.act_one_ref, ...), custom_call_target="tpu_custom_call" | custom-call | tf_op jit(solution)/shard_map/descend/pallas_call | solution.py:656
  395.0 1.0 copy.23
  395.9 0.7 slice.31
  396.6 1.7 slice_add_fusion
  399.0 1.9 copy.29
  400.9 1.9 copy.30
